TPU v7x, 32 devices: a whole 2x2x4 slice. The times are simulated.
32 devices in a mesh: section: 4 (over y, x), seq: 2 (over core), dp: 4 (over z).
Axes of the slice: x: 2, y: 2, z: 4, core: 2. Of those that a mesh axis runs over, the one named last changes fastest.
Arguments:
- stream: bfloat16 [4, 4, 256, 1280], P('section', 'dp', 'seq'), may hold values from -16 to 16
- norm_gain: float32 [4, 1280], P('section'), may hold values from 0.25 to 1.75
- w_xbc: bfloat16 [4, 1280, 2688], P('section', ('seq', 'dp')), may hold values from -0.15625 to 0.15625
- w_dt: bfloat16 [4, 1280, 40], P('section', ('seq', 'dp')), may hold values from -0.15625 to 0.15625
- conv_weight: float32 [4, 4, 2688], P('section'), may hold values from -3 to 3
- conv_bias: float32 [4, 2688], P('section'), may hold values from -1.8 to 1.8
- dt_bias: float32 [4, 40], P('section'), may hold values from -1 to 1
- decay_rate: float32 [4, 40], P('section'), may hold values from 0.000390625 to 0.04
- skip_weight: float32 [4, 40], P('section'), may hold values from 0.5 to 1.5
- inner_gain: float32 [4, 2560], P('section'), may hold values from 0.25 to 1.75
- w_out: bfloat16 [4, 2560, 1280], P('section', ('seq', 'dp')), may hold values from -0.125 to 0.125
Outputs:
- next_stream: bfloat16 [4, 4, 256, 1280], P('section', 'dp', 'seq')
All inputs are finite; a program needn't handle non-finite values.
Results may differ from a plain program's by a relative error of at most 0.008.
Values may be sent and summed in bfloat16 or wider, within the bound.
A program may use at most 64 MiB of HBM per device.

v0:
```python
import functools

import jax
import jax.numpy as jnp
from jax import lax
from jax.experimental import pallas as pl
from jax.experimental.pallas import tpu as pltpu
from jax.sharding import PartitionSpec as P

HEADS = 40
HEAD_DIM = 64
STATE = 64
CONV = 4
BLOCK = 128
INNER = 2560


epsilon = 1e-05


def prefix(x, axis, combine, identity):
    devices, position = (lax.axis_size(axis), lax.axis_index(axis))
    everything = jax.tree.map(
        lambda part, kind: lax.all_gather(part.astype(kind), axis),
        x,
        jax.tree.map(lambda a: jnp.bfloat16 if a.dtype == jnp.float32 else a.dtype, x),
    )
    start = jax.tree.map(
        lambda part, zero: jnp.broadcast_to(jnp.asarray(zero, part.dtype), part.shape), x, identity
    )

    def hop(k, before):
        reached = k < position
        new = combine(
            before, jax.tree.map(lambda part, own: part[k].astype(own.dtype), everything, x)
        )
        return jax.tree.map(lambda a, b: jnp.where(reached, a, b), new, before)

    return lax.fori_loop(0, devices, hop, start)


def from_behind(x, axis, by):
    devices = lax.axis_size(axis)
    pairs = [(i, i + by) for i in range(devices) if 0 <= i + by < devices]
    return lax.ppermute(x, axis, pairs)


def passed_along(x, axis, by):
    devices = lax.axis_size(axis)
    return lax.ppermute(x, axis, [(i, (i + by) % devices) for i in range(devices)])


def rms_scale(values, scale_gain):
    mean_square = jnp.mean(values * values, axis=-1, keepdims=True)
    return values * lax.rsqrt(mean_square + epsilon) * scale_gain


def block_terms(values, b_rows, c_rows, dt_rows, head_rates):
    block_len = dt_rows.shape[0]
    cum_decay = jnp.cumsum(-dt_rows * head_rates[None, :], axis=0)
    scores = jnp.dot(c_rows, b_rows.T, preferred_element_type=jnp.float32)
    lag_decay = cum_decay.T[:, :, None] - cum_decay.T[:, None, :]
    causal = jnp.arange(block_len)[:, None] >= jnp.arange(block_len)[None, :]
    weights = jnp.where(causal[None], jnp.exp(jnp.minimum(lag_decay, 0.0)), 0.0)
    mixing = (scores[None] * weights * dt_rows.T[:, None, :]).astype(jnp.bfloat16)
    intra_out = jnp.einsum("hij,jhp->ihp", mixing, values, preferred_element_type=jnp.float32)
    tail_weight = jnp.exp(cum_decay[-1][None, :] - cum_decay) * dt_rows
    scaled = (values.astype(jnp.float32) * tail_weight[:, :, None]).astype(jnp.bfloat16)
    summary = jnp.einsum("jhp,jn->hpn", scaled, b_rows, preferred_element_type=jnp.float32)
    return (intra_out, summary, jnp.exp(cum_decay[-1]), jnp.exp(cum_decay))


def state_output(c_rows, growth, carried):
    readout = jnp.einsum(
        "in,hpn->ihp", c_rows.astype(jnp.float32), carried, precision=lax.Precision.HIGHEST
    )
    return growth[:, :, None] * readout


def combine_states(earlier, latest):
    decay_a, state_a = earlier
    decay_b, state_b = latest
    return (decay_a * decay_b, decay_b[:, None] * state_a + state_b)


def chain_states(summary):
    identity = (jnp.ones_like(summary[0]), jnp.zeros_like(summary[1]))
    return prefix(summary, "seq", combine_states, identity)


def project_rows(normed_rows, xbc_part, dt_part):
    return (
        jnp.dot(
            normed_rows,
            lax.all_gather(xbc_part, ("seq", "dp"), axis=0, tiled=True),
            preferred_element_type=jnp.float32,
        ),
        jnp.dot(
            normed_rows,
            lax.all_gather(dt_part, ("seq", "dp"), axis=0, tiled=True),
            preferred_element_type=jnp.float32,
        ),
    )


def shards(
    stream,
    norm_gain,
    w_xbc,
    w_dt,
    conv_weight,
    conv_bias,
    dt_bias,
    decay_rate,
    skip_weight,
    inner_gain,
    w_out,
):
    rows_in = stream[0, 0]
    length_dev = rows_in.shape[0]
    margin = CONV - 1
    row_gain = norm_gain[0]
    normed = rms_scale(rows_in.astype(jnp.float32), row_gain).astype(jnp.bfloat16)
    projected, dt_raw = project_rows(normed, w_xbc[0], w_dt[0])
    xbc_raw = projected.astype(jnp.bfloat16)
    prev_proj = from_behind(xbc_raw[length_dev - margin :], "seq", 1)
    padded = jnp.concatenate([prev_proj, xbc_raw], axis=0)
    conv_sum = jnp.broadcast_to(conv_bias[0][None, :], (length_dev, padded.shape[1]))
    for tap_index in range(CONV):
        conv_sum = conv_sum + conv_weight[0, tap_index][None, :] * padded[
            tap_index : tap_index + length_dev
        ].astype(jnp.float32)
    mixed_rows = jax.nn.silu(conv_sum).astype(jnp.bfloat16)
    blocks = length_dev // BLOCK
    values = mixed_rows[:, :INNER].reshape(blocks, BLOCK, HEADS, HEAD_DIM)
    b_rows = mixed_rows[:, INNER : INNER + STATE].reshape(blocks, BLOCK, STATE)
    c_rows = mixed_rows[:, INNER + STATE :].reshape(blocks, BLOCK, STATE)
    dt_rows = jax.nn.softplus(dt_raw + dt_bias[0][None, :]).reshape(blocks, BLOCK, HEADS)
    intra_out, summary, totals, growth = jax.vmap(block_terms, in_axes=(0, 0, 0, 0, None))(
        values, b_rows, c_rows, dt_rows, decay_rate[0]
    )

    def local_step(running, inputs):
        carried, decay_before = running
        block_total, block_summary = inputs
        return (
            (block_total[:, None, None] * carried + block_summary, decay_before * block_total),
            (carried, decay_before),
        )

    start_state = (
        jnp.zeros((HEADS, HEAD_DIM, STATE), jnp.float32),
        jnp.ones((HEADS,), jnp.float32),
    )
    (local_state, local_decay), (enter_local, decay_before) = lax.scan(
        local_step, start_state, (totals, summary)
    )
    state_terms = jax.vmap(state_output)
    early_terms = state_terms(c_rows, growth, enter_local)
    incoming_decay, incoming_flat = chain_states(
        (local_decay, local_state.reshape(HEADS, HEAD_DIM * STATE))
    )
    arriving = incoming_flat.reshape(HEADS, HEAD_DIM, STATE)
    late_terms = state_terms(c_rows, growth, decay_before[:, :, None, None] * arriving[None])
    state_part = early_terms + late_terms
    mixed_out = (
        intra_out + state_part + skip_weight[0][None, None, :, None] * values.astype(jnp.float32)
    )
    normed_out = rms_scale(mixed_out.reshape(length_dev, INNER), inner_gain[0]).astype(jnp.bfloat16)
    branch_out = jnp.dot(
        normed_out,
        lax.all_gather(w_out[0], ("seq", "dp"), axis=0, tiled=True),
        preferred_element_type=jnp.float32,
    )
    next_rows = (rows_in.astype(jnp.float32) + branch_out).astype(jnp.bfloat16)
    shifted = passed_along(next_rows, "section", 1)
    return shifted[None, None]

def section_kernel(
    Z, x_hbm, ng_ref, w_hbm, wd_ref, cw_ref, cb_ref, db_ref, dr_ref, sk_ref, ig_ref, wo_hbm,
    out_ref,
    x_ref, w_ref, wo_ref, w2, wbuf, d2, dbuf, wobuf, sbuf, nbuf, cbuf, vbuf, ybuf, state,
    pbuf, stbuf, xpart, xstat, bpart, bstat, rpart, rstat, obuf,
    l_sem, w_send, w_recv, d_send, d_recv, f_send, f_recv, g_send, g_recv, o_send, o_recv,
    s_send, s_recv, h_send, p_send, p_recv, t_send, t_recv, x_recv, y_recv, b_send, c_send, q_send, b_recv,
    e_send, e_recv,
):
    z = lax.axis_index("dp")
    c = lax.axis_index("seq")
    sec = lax.axis_index("section")
    NS = lax.axis_size("section")
    nxt = lax.rem(sec + 1, NS)
    prv = lax.rem(sec + NS - 1, NS)
    S = Z // 2
    rows, D = x_ref.shape
    KR = w_ref.shape[0]
    per = INNER // (2 * Z)
    hper = HEADS // (2 * Z)
    VC = 2 * per
    NB = 2 * STATE
    CC = VC + NB
    f32, bf16 = jnp.float32, jnp.bfloat16
    own_core = lax.rem(z, 2) == c
    myslot = z // 2
    sib = {"seq": 1 - c}
    upper = z >= S
    border = jnp.where(upper, S, S - 1)

    def rcopy(src, dst, ss, rs, where):
        return pltpu.make_async_remote_copy(
            src_ref=src, dst_ref=dst, send_sem=ss, recv_sem=rs, device_id=where,
            device_id_type=pl.DeviceIdType.MESH,
        )

    loads = [
        pltpu.make_async_copy(src, dst, l_sem.at[i])
        for i, (src, dst) in enumerate(((x_hbm, x_ref), (w_hbm, w_ref), (wo_hbm, wo_ref)))
    ]
    for load in loads:
        load.start()
    barrier = pltpu.get_barrier_semaphore()
    for d in range(Z):
        for e in range(2):
            @pl.when(jnp.logical_not(jnp.logical_and(d == z, e == c)))
            def _():
                pl.semaphore_signal(barrier, inc=1, device_id={"dp": d, "seq": e},
                                    device_id_type=pl.DeviceIdType.MESH)
    for s in (nxt, prv):
        pl.semaphore_signal(barrier, inc=1, device_id={"section": s},
                            device_id_type=pl.DeviceIdType.MESH)

    def row0(core, chip):
        return pl.multiple_of((core * Z + chip) * KR, KR)

    lanes = d2.shape[2]
    for d in range(Z):
        two = jnp.concatenate(
            [wd_ref[d * hper : (d + 1) * hper, :].astype(f32),
             wd_ref[(Z + d) * hper : (Z + d + 1) * hper, :].astype(f32),
             jnp.zeros((16 - 2 * hper, KR), f32)], axis=0)
        d2[d] = jnp.concatenate([two, jnp.zeros((16, lanes - KR), f32)], axis=1).astype(bf16)
    dbuf[c * Z + z] = d2[z]
    loads[0].wait()

    @pl.when(own_core)
    def _():
        sbuf[myslot, c] = x_ref[...]

    loads[1].wait()
    for d in range(Z):
        w2[d, :, 0:per] = w_ref[:, d * per : (d + 1) * per]
        w2[d, :, per:VC] = w_ref[:, Z * per + d * per : Z * per + (d + 1) * per]
        w2[d, :, VC:CC] = w_ref[:, INNER : INNER + NB]

    pl.semaphore_wait(barrier, 2 * Z - 1 + 2)

    def s_copy(src, k, h, direction):
        return rcopy(src, sbuf.at[k, h], s_send.at[k, h, direction], s_recv.at[k, h],
                     {"dp": z + (1 if direction else -1)})

    half_out = rcopy(x_ref, sbuf.at[myslot, c], h_send, s_recv.at[myslot, c], sib)

    @pl.when(jnp.logical_not(own_core))
    def _():
        half_out.start()

    def up_down(k, h, fn):
        b = 2 * k + c
        @pl.when(jnp.logical_and(z >= b, z + 1 < Z))
        def _():
            fn(s_copy(sbuf.at[k, h], k, h, 1))
        @pl.when(jnp.logical_and(z <= b, z > 0))
        def _():
            fn(s_copy(sbuf.at[k, h], k, h, 0))

    def own_halves(across):
        for h in (c, 1 - c):
            if not across:
                @pl.when(jnp.logical_and(own_core, h != c))
                def _():
                    s_copy(x_ref, myslot, h, 0).wait_recv()
            for direction, on, edge in ((1, z + 1 < Z, S - 1), (0, z > 0, S)):
                cross = z == edge
                go = cross if across else jnp.logical_not(cross)
                @pl.when(jnp.logical_and(jnp.logical_and(own_core, on), go))
                def _():
                    s_copy(sbuf.at[myslot, h], myslot, h, direction).start()

    own_halves(False)

    def w_copies(d, frm):
        at = pl.ds(row0(c, frm), KR)
        g = c * Z + frm
        return (rcopy(w2.at[d], wbuf.at[at], w_send.at[d], w_recv.at[frm], {"dp": d}),
                rcopy(d2.at[d], dbuf.at[g], d_send.at[d], d_recv.at[frm], {"dp": d}))

    def f_copies(d, core):
        at = pl.ds(row0(core, d), KR)
        g = core * Z + d
        return (rcopy(wbuf.at[at], wbuf.at[at], f_send.at[d], f_recv.at[d], sib),
                rcopy(dbuf.at[g], dbuf.at[g], g_send.at[d], g_recv.at[d], sib))

    for step in range(Z - 1, 0, -1):
        for d in (z + step, z - step):
            @pl.when(jnp.logical_and(d >= 0, d < Z))
            def _():
                for cp in w_copies(d, z):
                    cp.start()
    own_halves(True)
    own_fwd = (
        rcopy(w2.at[z], wbuf.at[pl.ds(row0(c, z), KR)], f_send.at[z], f_recv.at[z], sib),
        rcopy(d2.at[z], dbuf.at[c * Z + z], g_send.at[z], g_recv.at[z], sib),
    )
    for cp in own_fwd:
        cp.start()
    wbuf[pl.ds(row0(c, z), KR), :] = w2[z]
    loads[2].wait()
    at_wo = pl.ds(pl.multiple_of(c * per, per), per)
    wo_copy = rcopy(wo_ref, wobuf.at[at_wo], o_send, o_recv, sib)
    wo_copy.start()
    wobuf[at_wo, :] = wo_ref[...]

    near = jnp.where(upper, S - 1, 0)
    gain_in = ng_ref[...]

    def pass_on(k, h):
        @pl.when(jnp.logical_not(jnp.logical_and(own_core, k == myslot)))
        def _():
            s_copy(x_ref, k, h, 0).wait_recv()
            up_down(k, h, lambda cp: cp.start())

    def norm_in(k, h):
        v = sbuf[k, h].astype(f32)
        ms = jnp.mean(v * v, axis=-1, keepdims=True)
        nbuf[k, h] = (v * lax.rsqrt(ms + epsilon) * gain_in).astype(bf16)

    far = 1 - near
    for h in range(2):
        pass_on(near, h)
        norm_in(near, h)
    for step in range(1, Z):
        for d in (z + step, z - step):
            @pl.when(jnp.logical_and(d >= 0, d < Z))
            def _():
                for cp in w_copies(z, d):
                    cp.wait_recv()
                for cp in f_copies(d, c):
                    cp.start()

    def pick(ref, width, tail):
        wide = Z * width
        got = None
        for d in range(Z):
            part = jnp.concatenate(
                [ref[:, d * width : (d + 1) * width],
                 ref[:, wide + d * width : wide + (d + 1) * width]], axis=1)
            part = jnp.where(z == d, part, 0.0)
            got = part if got is None else got + part
        return jnp.concatenate([got, tail], axis=1) if tail is not None else got

    hi = lax.Precision.HIGHEST
    taps = pick(cw_ref, per, cw_ref[:, INNER : INNER + NB])
    tbias = pick(cb_ref, per, cb_ref[:, INNER : INNER + NB])
    hz = jnp.zeros((1, 128 - 2 * hper), f32)
    heads = jnp.concatenate(
        [pick(db_ref, hper, hz), pick(dr_ref, hper, hz), pick(sk_ref, hper, hz),
         jnp.zeros((5, 128), f32)], axis=0)
    heads_t = heads.T[0:16]
    dtb, rate = heads_t[:, 0:1], heads_t[:, 1:2]
    gain_out = pick(ig_ref, per, None)
    spread = (lax.broadcasted_iota(jnp.int32, (16, VC), 1) // HEAD_DIM
              == lax.broadcasted_iota(jnp.int32, (16, VC), 0)).astype(f32)

    def widen(m):
        return jnp.dot(m, spread, precision=hi, preferred_element_type=f32)

    skip_wide = widen(heads[:, 0:16])[2:3]
    ii = lax.broadcasted_iota(jnp.int32, (BLOCK, BLOCK), 0)
    jj = lax.broadcasted_iota(jnp.int32, (BLOCK, BLOCK), 1)
    causal = ii >= jj
    triu = (ii <= jj).astype(f32)
    low_lane = lax.broadcasted_iota(jnp.int32, (BLOCK, 128), 1) < HEAD_DIM
    margin = CONV - 1
    for d in range(Z):
        for cp in f_copies(d, 1 - c):
            cp.wait_recv()
    wo_copy.wait_recv()
    w_steps = jnp.concatenate([dbuf[g][:, 0:KR].astype(f32) for g in range(2 * Z)], axis=1).astype(bf16)

    def p_copies(k, h):
        b = 2 * k + c
        slot = lax.rem(z, S)
        return (rcopy(pbuf.at[k, h], rpart.at[slot], p_send.at[k, h], p_recv.at[slot], {"dp": b, "seq": h}),
                rcopy(stbuf.at[k, h], rstat.at[slot], t_send.at[k, h], t_recv.at[slot], {"dp": b, "seq": h}))

    half = rows // 2

    def x_copies(h, frm, q):
        slot = lax.rem(frm, S)
        at = pl.ds(q * half, half)
        big = rcopy(pbuf.at[far, h, at], xpart.at[slot, h, at], q_send.at[h, q], x_recv.at[slot, h, q], {"dp": border})
        if q > 0:
            return (big,)
        return (rcopy(stbuf.at[far, h], xstat.at[slot, h], t_send.at[far, h], y_recv.at[slot, h], {"dp": border}), big)

    def b_copies(h, q):
        where = {"dp": 2 * far + c, "seq": h}
        at = pl.ds(q * half, half)
        big = rcopy(bpart.at[h, at], rpart.at[S, at], b_send.at[h, q], b_recv.at[q], where)
        if q > 0:
            return (big,)
        return (rcopy(bstat.at[h], rstat.at[S], c_send.at[h], t_recv.at[S], where), big)

    def unit(k, h):
        nb = nbuf[k, h]
        if h == 0:
            cbuf[0:8, :] = jnp.zeros((8, CC), f32)
        else:
            cbuf[0:8, :] = cbuf[rows : rows + 8, :]
        cbuf[8 : 8 + rows, :] = jnp.dot(nb, wbuf[...], preferred_element_type=f32).astype(bf16).astype(f32)
        acc = jnp.broadcast_to(tbias, (rows, CC))
        for t in range(CONV):
            acc = acc + taps[t : t + 1, :] * cbuf[8 - margin + t : 8 - margin + t + rows, :]
        vbuf[...] = (acc / (1.0 + jnp.exp(-acc))).astype(bf16)
        raw = lax.dot_general(w_steps, nb, (((1,), (1,)), ((), ())), preferred_element_type=f32) + dtb
        dt_t = jnp.maximum(raw, 0.0) + jnp.log1p(jnp.exp(-jnp.abs(raw)))
        cum_t = jnp.dot(-dt_t * rate, triu, precision=hi, preferred_element_type=f32)
        tail_t = jnp.exp(cum_t[:, BLOCK - 1 : BLOCK] - cum_t) * dt_t
        cols = jnp.concatenate([cum_t, tail_t, jnp.exp(cum_t), jnp.zeros((80, BLOCK), f32)], axis=0).T
        cum = cols[:, 0:16]
        bm = vbuf[:, VC : VC + STATE]
        cm = vbuf[:, VC + STATE : CC]
        scores = lax.dot_general(cm, bm, (((1,), (1,)), ((), ())), preferred_element_type=f32)
        scores = jnp.where(causal, scores, 0.0)
        vals = vbuf[:, 0:VC].astype(f32)
        part = skip_wide * vals
        if h > 0:
            grow = widen(cols[:, 32:48])
            part = part + grow * jnp.dot(cm.astype(f32), state[...], precision=hi,
                                         preferred_element_type=f32)
        for p in range(VC // 128):
            mix = []
            for q in range(2):
                hd = 2 * p + q
                lag = cum[:, hd : hd + 1] - cum_t[hd : hd + 1, :]
                m = scores * jnp.exp(jnp.minimum(lag, 0.0)) * dt_t[hd : hd + 1, :]
                mix.append(m.astype(bf16))
            vp = vals[:, p * 128 : (p + 1) * 128]
            two = jnp.concatenate([jnp.where(low_lane, vp, 0.0), jnp.where(low_lane, 0.0, vp)],
                                  axis=0).astype(bf16)
            got = jnp.dot(jnp.concatenate(mix, axis=1), two, preferred_element_type=f32)
            ybuf[:, p * 128 : (p + 1) * 128] = got + part[:, p * 128 : (p + 1) * 128]
        y = ybuf[...]
        pbuf[k, h] = jnp.dot((y * gain_out).astype(bf16), wobuf[...], preferred_element_type=f32).astype(bf16)
        stbuf[k, h] = lax.dot_general(jnp.ones((8, VC), f32), y * y, (((1,), (1,)), ((), ())),
                                      precision=hi, preferred_element_type=f32)
        if h == 0:
            scaled = (vals * widen(cols[:, 16:32])).astype(bf16)
            state[...] = lax.dot_general(bm, scaled, (((0,), (0,)), ((), ())), preferred_element_type=f32)

    def send_far(h):
        @pl.when(z != border)
        def _():
            for q in range(2):
                for cp in x_copies(h, z, q):
                    cp.start()

    def sum_far(h):
        @pl.when(z == border)
        def _():
            for q in range(2):
                r = slice(q * half, (q + 1) * half)
                total = pbuf[far, h, r].astype(f32)
                stat = stbuf[far, h]
                for j in range(S):
                    frm = jnp.where(upper, S + j, j)
                    @pl.when(frm != border)
                    def _():
                        for cp in x_copies(h, frm, q):
                            cp.wait_recv()
                    total = total + jnp.where(frm == border, 0.0, xpart[j, h, r].astype(f32))
                    stat = stat + jnp.where(frm == border, 0.0, xstat[j, h])
                bpart[h, r] = total.astype(bf16)
                if q == 0:
                    bstat[h] = stat
                for cp in b_copies(h, q):
                    cp.start()

    def here(k, h):
        return jnp.logical_and(2 * k + c == z, h == c)

    def send_near(h, now):
        @pl.when(jnp.logical_and(now, here(near, h)))
        def _():
            rpart[lax.rem(z, S)] = pbuf[near, h]
            rstat[lax.rem(z, S)] = stbuf[near, h]

        @pl.when(jnp.logical_and(now, jnp.logical_not(here(near, h))))
        def _():
            for cp in p_copies(near, h):
                cp.start()

    for h in range(2):
        unit(near, h)
        send_near(h, z != border)
    for h in range(2):
        pass_on(far, h)
        norm_in(far, h)
        unit(far, h)
        send_far(h)
    for h in range(2):
        send_near(h, z == border)
    for h in range(2):
        sum_far(h)

    total = jnp.zeros((rows, D), f32)
    stat = jnp.zeros((8, rows), f32)
    for j in range(S + 1):
        mine = jnp.logical_and(own_core, lax.rem(z, S) == j) if j < S else False
        @pl.when(jnp.logical_not(mine))
        def _():
            if j == S:
                for q in range(2):
                    at = pl.ds(q * half, half)
                    rcopy(pbuf.at[0, 0, at], rpart.at[S, at], b_send.at[0, q], b_recv.at[q], sib).wait_recv()
            else:
                rcopy(pbuf.at[0, 0], rpart.at[j], p_send.at[0, 0], p_recv.at[j], sib).wait_recv()
            rcopy(stbuf.at[0, 0], rstat.at[j], t_send.at[0, 0], t_recv.at[j], sib).wait_recv()
        total = total + rpart[j].astype(f32)
        stat = stat + rstat[j]
    scale = lax.rsqrt(stat * (1.0 / INNER) + epsilon).T[:, 0:1]
    obuf[...] = (x_ref[...].astype(f32) + total * scale).astype(bf16)
    last_copy = rcopy(obuf, out_ref, e_send, e_recv, {"section": nxt})
    last_copy.start()

    @pl.when(jnp.logical_not(own_core))
    def _():
        half_out.wait_send()
    for cp in (*own_fwd, wo_copy):
        cp.wait_send()
    for d in range(Z):
        @pl.when(d != z)
        def _():
            for cp in (*w_copies(d, z), *f_copies(d, c)):
                cp.wait_send()
    for h in range(2):
        for k in range(S):
            up_down(k, h, lambda cp: cp.wait_send())
        @pl.when(z != border)
        def _():
            for cp in (*x_copies(h, z, 0), *x_copies(h, z, 1)):
                cp.wait_send()
        @pl.when(z == border)
        def _():
            for cp in (*b_copies(h, 0), *b_copies(h, 1)):
                cp.wait_send()
        @pl.when(jnp.logical_not(here(near, h)))
        def _():
            for cp in p_copies(near, h):
                cp.wait_send()
    last_copy.wait()


def fused(
    stream, norm_gain, w_xbc, w_dt, conv_weight, conv_bias, dt_bias, decay_rate, skip_weight,
    inner_gain, w_out,
):
    Z = lax.axis_size("dp")
    rows, D = stream.shape[2:]
    if rows != BLOCK:
        return shards(stream, norm_gain, w_xbc, w_dt, conv_weight, conv_bias, dt_bias, decay_rate,
                      skip_weight, inner_gain, w_out)
    KR = w_xbc.shape[1]
    VC = INNER // Z
    CC = VC + 2 * STATE
    S = Z // 2
    lanes = -(-KR // 128) * 128
    bf16, f32 = jnp.bfloat16, jnp.float32
    dma, V = pltpu.SemaphoreType.DMA, pltpu.VMEM
    far, held = pl.BlockSpec(memory_space=pl.ANY), pl.BlockSpec(memory_space=pltpu.VMEM)
    out = pl.pallas_call(
        functools.partial(section_kernel, Z),
        out_shape=jax.ShapeDtypeStruct((rows, D), bf16),
        in_specs=[far, held, far] + [held] * 7 + [far],
        out_specs=held,
        scratch_shapes=[
            V((rows, D), bf16), V(w_xbc.shape[1:], bf16), V(w_out.shape[1:], bf16),
            V((Z, KR, CC), bf16), V((2 * Z * KR, CC), bf16),
            V((Z, 16, lanes), bf16), V((2 * Z, 16, lanes), bf16),
            V((VC, D), bf16),
            V((S, 2, rows, D), bf16), V((S, 2, rows, D), bf16),
            V((8 + rows, CC), f32), V((rows, CC), bf16), V((rows, VC), f32), V((STATE, VC), f32),
            V((S, 2, rows, D), bf16), V((S, 2, 8, rows), f32),
            V((S, 2, rows, D), bf16), V((S, 2, 8, rows), f32),
            V((2, rows, D), bf16), V((2, 8, rows), f32),
            V((S + 1, rows, D), bf16), V((S + 1, 8, rows), f32),
            V((rows, D), bf16),
            dma((3,)), dma((Z,)), dma((Z,)), dma((Z,)), dma((Z,)), dma((Z,)), dma((Z,)), dma((Z,)),
            dma((Z,)), dma, dma, dma((S, 2, 2)), dma((S, 2)), dma, dma((S, 2)), dma((S + 1,)),
            dma((S, 2)), dma((S + 1,)), dma((S, 2, 2)), dma((S, 2)), dma((2, 2)), dma((2,)), dma((2, 2)), dma((2,)), dma, dma,
        ],
        compiler_params=pltpu.CompilerParams(
            collective_id=0, has_side_effects=True, vmem_limit_bytes=50 * 1024 * 1024
        ),
    )(
        stream[0, 0], norm_gain, w_xbc[0], jnp.swapaxes(w_dt, 1, 2)[0], conv_weight[0], conv_bias,
        dt_bias, decay_rate, skip_weight, inner_gain, w_out[0],
    )
    return out[None, None]


def solution(mesh):
    placed = (
        P("section", "dp", "seq", None),
        P("section", None),
        P("section", ("seq", "dp"), None),
        P("section", ("seq", "dp"), None),
        P("section", None, None),
        P("section", None),
        P("section", None),
        P("section", None),
        P("section", None),
        P("section", None),
        P("section", ("seq", "dp"), None),
    )
    size = mesh.shape
    chips = size["dp"]
    whole_heads = HEADS % (2 * chips) == 0 and (INNER // chips) % 128 == 0
    body = fused if size["seq"] == 2 and chips == 4 and whole_heads and size["section"] > 1 else shards
    return jax.shard_map(
        body,
        mesh=mesh,
        in_specs=placed,
        out_specs=P("section", "dp", "seq", None),
        check_vma=False,
    )
```

profile of v0, /device:TPU:1, one launch (start us, length us, event | category | flops | bytes accessed | tf_op | source)
XLA Modules:
  0.0 86.2 jit_solution(18340762983352168368)
XLA Ops:
  0.0 0.0 copy-start.7
  0.0 0.0 copy-start.8
  0.0 0.0 copy-start.9
  0.0 0.0 copy-start.10
  0.0 0.7 copy-done.7
  0.7 0.0 copy-done.8
  0.7 0.0 copy-done.9
  0.7 0.0 copy-done.10
  0.7 0.0 copy-start
  0.7 1.2 %copy-done = bf16[1,160,2688]{2,1,0:T(8,128)(2,1)S(1)} copy-done((bf16[1,160,2688]{2,1,0:T(8,128)(2,1)S(1)}, bf16[1,160,2688]{2,1,0:T(8,128)(2,1)}, u32[]{:S(2)}) %copy-start) | copy-done | bytes 860184
  1.9 0.0 copy-start.1
  1.9 1.1 %copy-done.1 = bf16[1,320,1280]{2,1,0:T(8,128)(2,1)S(1)} copy-done((bf16[1,320,1280]{2,1,0:T(8,128)(2,1)S(1)}, bf16[1,320,1280]{2,1,0:T(8,128)(2,1)}, u32[]{:S(2)}) %copy-start.1) | copy-done | bytes 819224
  3.0 0.0 copy-start.2
  3.0 1.0 %copy-done.2 = bf16[1,1,128,1280]{3,2,1,0:T(8,128)(2,1)S(1)} copy-done((bf16[1,1,128,1280]{3,2,1,0:T(8,128)(2,1)S(1)}, bf16[1,1,128,1280]{3,2,1,0:T(8,128)(2,1)}, u32[]{:S(2)}) %copy-start.2) | copy-done | bytes 327704
  4.0 0.0 copy-start.3
  4.0 0.8 copy-done.3
  4.8 0.0 copy-start.4
  4.8 0.7 copy-done.4
  5.5 0.0 copy-start.5
  5.5 0.7 copy-done.5
  6.2 0.0 copy-start.6
  6.2 0.7 copy-done.6
  6.9 78.6 %shard_map.109 = bf16[128,1280]{1,0:T(8,128)(2,1)S(1)} custom-call(bf16[128,1280]{1,0:T(8,128)(2,1)S(1)} %bitcast.11, f32[1,1280]{1,0:T(1,128)S(1)} %copy-done.7, bf16[160,2688]{1,0:T(8,128)(2,1)S(1)} %bitcast.9, bf16[40,160]{1,0:T(8,128)(2,1)S(1)} %bitcast.13, f32[4,2688]{1,0:T(4,128)S(1)} %bitcast.12, f32[1,2688]{1,0:T(1,128)S(1)} %copy-done.5, ...), custom_call_target="tpu_custom_call" | custom-call | tf_op jit(solution)/shard_map/pallas_call | solution.py:581
  85.5 0.7 copy.13
Async XLA Ops:
  0.0 0.7 copy-start.7
  0.0 0.7 copy-start.8
  0.0 0.7 copy-start.9
  0.0 0.7 copy-start.10
  0.7 1.2 %copy-start = (bf16[1,160,2688]{2,1,0:T(8,128)(2,1)S(1)}, bf16[1,160,2688]{2,1,0:T(8,128)(2,1)}, u32[]{:S(2)}) copy-start(bf16[1,160,2688]{2,1,0:T(8,128)(2,1)} %param.13) | copy-start | bytes 2580484
  1.9 1.1 %copy-start.1 = (bf16[1,320,1280]{2,1,0:T(8,128)(2,1)S(1)}, bf16[1,320,1280]{2,1,0:T(8,128)(2,1)}, u32[]{:S(2)}) copy-start(bf16[1,320,1280]{2,1,0:T(8,128)(2,1)} %param.21) | copy-start | bytes 2457604
  3.0 1.0 %copy-start.2 = (bf16[1,1,128,1280]{3,2,1,0:T(8,128)(2,1)S(1)}, bf16[1,1,128,1280]{3,2,1,0:T(8,128)(2,1)}, u32[]{:S(2)}) copy-start(bf16[1,1,128,1280]{3,2,1,0:T(8,128)(2,1)} %param.11) | copy-start | bytes 983044
  4.0 0.8 copy-start.3
  4.8 0.7 copy-start.4
  5.5 0.7 copy-start.5
  6.2 0.7 copy-start.6
where the time goes:
time: 86.9 us; the launch traced here: 86.2 us
  Pallas kernels  78.6 us (90%)
  local copies, waits for them, and re-layouts  7.6 us (9%)
    pallas_call x1, Pallas kernels, fused(): pl.pallas_call(functools.partial(section_kernel, Z), out_shape=jax.ShapeD...  78.6 us
    unnamed x23, local copies, waits for them, and re-layouts  7.6 us

commit v1 on v0

--- a/solution.py
+++ b/solution.py
@@ -177,9 +177,9 @@
     return shifted[None, None]
 
 def section_kernel(
-    Z, x_hbm, ng_ref, w_hbm, wd_ref, cw_ref, cb_ref, db_ref, dr_ref, sk_ref, ig_ref, wo_hbm,
+    Z, x_hbm, ng_hbm, w_hbm, wd_hbm, cw_hbm, cb_hbm, db_hbm, dr_hbm, sk_hbm, ig_hbm, wo_hbm,
     out_ref,
-    x_ref, w_ref, wo_ref, w2, wbuf, d2, dbuf, wobuf, sbuf, nbuf, cbuf, vbuf, ybuf, state,
+    x_ref, ng_ref, w_ref, wd_ref, cw_ref, cb_ref, db_ref, dr_ref, sk_ref, ig_ref, wo_ref, w2, wbuf, d2, dbuf, wobuf, sbuf, nbuf, cbuf, vbuf, ybuf, state,
     pbuf, stbuf, xpart, xstat, bpart, bstat, rpart, rstat, obuf,
     l_sem, w_send, w_recv, d_send, d_recv, f_send, f_recv, g_send, g_recv, o_send, o_recv,
     s_send, s_recv, h_send, p_send, p_recv, t_send, t_recv, x_recv, y_recv, b_send, c_send, q_send, b_recv,
@@ -214,7 +214,10 @@
 
     loads = [
         pltpu.make_async_copy(src, dst, l_sem.at[i])
-        for i, (src, dst) in enumerate(((x_hbm, x_ref), (w_hbm, w_ref), (wo_hbm, wo_ref)))
+        for i, (src, dst) in enumerate((
+            (x_hbm, x_ref), (w_hbm, w_ref), (wd_hbm, wd_ref), (wo_hbm, wo_ref), (ng_hbm, ng_ref),
+            (cw_hbm, cw_ref), (cb_hbm, cb_ref), (db_hbm, db_ref), (dr_hbm, dr_ref), (sk_hbm, sk_ref),
+            (ig_hbm, ig_ref)))
     ]
     for load in loads:
         load.start()
@@ -233,6 +236,7 @@
         return pl.multiple_of((core * Z + chip) * KR, KR)
 
     lanes = d2.shape[2]
+    loads[2].wait()
     for d in range(Z):
         two = jnp.concatenate(
             [wd_ref[d * hper : (d + 1) * hper, :].astype(f32),
@@ -314,13 +318,15 @@
     for cp in own_fwd:
         cp.start()
     wbuf[pl.ds(row0(c, z), KR), :] = w2[z]
-    loads[2].wait()
+    loads[3].wait()
     at_wo = pl.ds(pl.multiple_of(c * per, per), per)
     wo_copy = rcopy(wo_ref, wobuf.at[at_wo], o_send, o_recv, sib)
     wo_copy.start()
     wobuf[at_wo, :] = wo_ref[...]
 
     near = jnp.where(upper, S - 1, 0)
+    for load in loads[4:]:
+        load.wait()
     gain_in = ng_ref[...]
 
     def pass_on(k, h):
@@ -577,14 +583,17 @@
     lanes = -(-KR // 128) * 128
     bf16, f32 = jnp.bfloat16, jnp.float32
     dma, V = pltpu.SemaphoreType.DMA, pltpu.VMEM
-    far, held = pl.BlockSpec(memory_space=pl.ANY), pl.BlockSpec(memory_space=pltpu.VMEM)
+    far, held = pl.BlockSpec(memory_space=pltpu.HBM), pl.BlockSpec(memory_space=pltpu.VMEM)
     out = pl.pallas_call(
         functools.partial(section_kernel, Z),
         out_shape=jax.ShapeDtypeStruct((rows, D), bf16),
-        in_specs=[far, held, far] + [held] * 7 + [far],
+        in_specs=[far] * 11,
         out_specs=held,
         scratch_shapes=[
-            V((rows, D), bf16), V(w_xbc.shape[1:], bf16), V(w_out.shape[1:], bf16),
+            V((rows, D), bf16), V(norm_gain.shape, f32), V(w_xbc.shape[1:], bf16),
+            V((HEADS, KR), bf16), V(conv_weight.shape[1:], f32), V(conv_bias.shape, f32),
+            V(dt_bias.shape, f32), V(dt_bias.shape, f32), V(dt_bias.shape, f32),
+            V(inner_gain.shape, f32), V(w_out.shape[1:], bf16),
             V((Z, KR, CC), bf16), V((2 * Z * KR, CC), bf16),
             V((Z, 16, lanes), bf16), V((2 * Z, 16, lanes), bf16),
             V((VC, D), bf16),
@@ -595,12 +604,12 @@
             V((2, rows, D), bf16), V((2, 8, rows), f32),
             V((S + 1, rows, D), bf16), V((S + 1, 8, rows), f32),
             V((rows, D), bf16),
-            dma((3,)), dma((Z,)), dma((Z,)), dma((Z,)), dma((Z,)), dma((Z,)), dma((Z,)), dma((Z,)),
+            dma((11,)), dma((Z,)), dma((Z,)), dma((Z,)), dma((Z,)), dma((Z,)), dma((Z,)), dma((Z,)),
             dma((Z,)), dma, dma, dma((S, 2, 2)), dma((S, 2)), dma, dma((S, 2)), dma((S + 1,)),
             dma((S, 2)), dma((S + 1,)), dma((S, 2, 2)), dma((S, 2)), dma((2, 2)), dma((2,)), dma((2, 2)), dma((2,)), dma, dma,
         ],
         compiler_params=pltpu.CompilerParams(
-            collective_id=0, has_side_effects=True, vmem_limit_bytes=50 * 1024 * 1024
+            collective_id=0, has_side_effects=True, vmem_limit_bytes=67043328
         ),
     )(
         stream[0, 0], norm_gain, w_xbc[0], jnp.swapaxes(w_dt, 1, 2)[0], conv_weight[0], conv_bias,

time: 86.9 us -> 81.7 us (0.940)
  local copies, waits for them, and re-layouts: 7.6 us -> 1.72 us
    unnamed x23 -> x1, local copies, waits for them, and re-layouts: 7.6 us -> 1.72 us
where the time goes in v1:
time: 81.7 us; the launch traced here: 80.7 us
  Pallas kernels  79 us (97%)
  local copies, waits for them, and re-layouts  1.72 us (2%)
    pallas_call x1, Pallas kernels, fused(): pl.pallas_call(functools.partial(section_kernel, Z), out_shape=jax.ShapeD...  79 us
    unnamed x1, local copies, waits for them, and re-layouts  1.72 us

profile of v1, /device:TPU:1, one launch (start us, length us, event | category | flops | bytes accessed | tf_op | source)
XLA Modules:
  0.0 80.7 jit_solution(1861491096386980036)
XLA Ops:
  0.0 79.0 %shard_map.109 = bf16[128,1280]{1,0:T(8,128)(2,1)} custom-call(bf16[128,1280]{1,0:T(8,128)(2,1)} %bitcast.11, f32[1,1280]{1,0:T(1,128)} %ng_hbm.1, bf16[160,2688]{1,0:T(8,128)(2,1)} %bitcast.9, bf16[40,160]{1,0:T(8,128)(2,1)} %bitcast.13, f32[4,2688]{1,0:T(4,128)} %bitcast.12, f32[1,2688]{1,0:T(1,128)} %cb_hbm.1, f32[1,40]{1,0:T(1,128)} %db_hbm.1, ...), custom_call_target="tpu_custom_call" | custom-call | tf_op jit(solution)/shard_map/pallas_call | solution.py:587
  79.0 1.7 %copy.13 = bf16[1,1,128,1280]{3,2,1,0:T(8,128)(2,1)} copy(bf16[1,1,128,1280]{3,2,1,0:T(8,128)(2,1)} %bitcast.8) | data formatting | bytes 655360

commit v2 on v1

--- a/solution.py
+++ b/solution.py
@@ -16,6 +16,8 @@
 
 
 epsilon = 1e-05
+QX = 4
+QP = 4
 
 
 def prefix(x, axis, combine, identity):
@@ -179,11 +181,12 @@
 def section_kernel(
     Z, x_hbm, ng_hbm, w_hbm, wd_hbm, cw_hbm, cb_hbm, db_hbm, dr_hbm, sk_hbm, ig_hbm, wo_hbm,
     out_ref,
-    x_ref, ng_ref, w_ref, wd_ref, cw_ref, cb_ref, db_ref, dr_ref, sk_ref, ig_ref, wo_ref, w2, wbuf, d2, dbuf, wobuf, sbuf, nbuf, cbuf, vbuf, ybuf, state,
+    x_ref, ng_ref, w_ref, wd_ref, cw_ref, cb_ref, db_ref, dr_ref, sk_ref, ig_ref, wo_ref, w2,
+    wbuf, d2, dbuf, wobuf, sbuf, nbuf, cbuf, tails, vbuf, ybuf, state,
     pbuf, stbuf, xpart, xstat, bpart, bstat, rpart, rstat, obuf,
     l_sem, w_send, w_recv, d_send, d_recv, f_send, f_recv, g_send, g_recv, o_send, o_recv,
-    s_send, s_recv, h_send, p_send, p_recv, t_send, t_recv, x_recv, y_recv, b_send, c_send, q_send, b_recv,
-    e_send, e_recv,
+    i_send, s_send, s_recv, e_send, e_recv, p_send, p_recv, t_send, t_recv,
+    q_send, x_recv, y_recv, b_send, c_send,
 ):
     z = lax.axis_index("dp")
     c = lax.axis_index("seq")
@@ -200,17 +203,25 @@
     NB = 2 * STATE
     CC = VC + NB
     f32, bf16 = jnp.float32, jnp.bfloat16
-    own_core = lax.rem(z, 2) == c
+    core = lax.rem(z, 2)
+    own_core = core == c
     myslot = z // 2
     sib = {"seq": 1 - c}
     upper = z >= S
     border = jnp.where(upper, S, S - 1)
+    edge = jnp.where(upper, Z - 1, 0)
+    near = jnp.where(upper, S - 1, 0)
+    far = 1 - near
+    scope = jax.named_scope
 
     def rcopy(src, dst, ss, rs, where):
         return pltpu.make_async_remote_copy(
             src_ref=src, dst_ref=dst, send_sem=ss, recv_sem=rs, device_id=where,
             device_id_type=pl.DeviceIdType.MESH,
         )
+
+    def band(q, parts):
+        return pl.ds(q * (rows // parts), rows // parts)
 
     loads = [
         pltpu.make_async_copy(src, dst, l_sem.at[i])
@@ -245,52 +256,60 @@
         d2[d] = jnp.concatenate([two, jnp.zeros((16, lanes - KR), f32)], axis=1).astype(bf16)
     dbuf[c * Z + z] = d2[z]
     loads[0].wait()
-
-    @pl.when(own_core)
-    def _():
-        sbuf[myslot, c] = x_ref[...]
-
     loads[1].wait()
     for d in range(Z):
         w2[d, :, 0:per] = w_ref[:, d * per : (d + 1) * per]
         w2[d, :, per:VC] = w_ref[:, Z * per + d * per : Z * per + (d + 1) * per]
         w2[d, :, VC:CC] = w_ref[:, INNER : INNER + NB]
 
-    pl.semaphore_wait(barrier, 2 * Z - 1 + 2)
-
-    def s_copy(src, k, h, direction):
-        return rcopy(src, sbuf.at[k, h], s_send.at[k, h, direction], s_recv.at[k, h],
-                     {"dp": z + (1 if direction else -1)})
-
-    half_out = rcopy(x_ref, sbuf.at[myslot, c], h_send, s_recv.at[myslot, c], sib)
-
-    @pl.when(jnp.logical_not(own_core))
-    def _():
-        half_out.start()
-
-    def up_down(k, h, fn):
+    with scope("barrier"):
+        pl.semaphore_wait(barrier, 2 * Z - 1 + 2)
+
+    def i_copy(q, way):
+        where = sib if way == 0 else {"dp": z + (1 if way == 1 else -1), "seq": core}
+        at = band(q, QX)
+        return rcopy(x_ref.at[at], sbuf.at[myslot, c, at], i_send.at[way, q], s_recv.at[myslot, c, q], where)
+
+    ways = ((0, jnp.logical_not(own_core)), (1, z + 1 < Z), (2, z > 0))
+
+    def send_x(on, inward):
+        for way, there in ways[1:]:
+            towards = jnp.logical_xor(upper, way == 1)
+            @pl.when(jnp.logical_and(jnp.logical_and(on, there), towards if inward else jnp.logical_not(towards)))
+            def _():
+                for q in range(QX):
+                    i_copy(q, way).start()
+
+    def s_copy(k, h, q, up):
+        at = band(q, QX)
+        return rcopy(sbuf.at[k, h, at], sbuf.at[k, h, at], s_send.at[k, h, q], s_recv.at[k, h, q],
+                     {"dp": z + (1 if up else -1)})
+
+    def relay(k, h, q, fn):
         b = 2 * k + c
-        @pl.when(jnp.logical_and(z >= b, z + 1 < Z))
+        @pl.when(jnp.logical_and(z > b, z + 1 < Z))
         def _():
-            fn(s_copy(sbuf.at[k, h], k, h, 1))
-        @pl.when(jnp.logical_and(z <= b, z > 0))
+            fn(s_copy(k, h, q, True))
+        @pl.when(jnp.logical_and(z < b, z > 0))
         def _():
-            fn(s_copy(sbuf.at[k, h], k, h, 0))
-
-    def own_halves(across):
-        for h in (c, 1 - c):
-            if not across:
-                @pl.when(jnp.logical_and(own_core, h != c))
-                def _():
-                    s_copy(x_ref, myslot, h, 0).wait_recv()
-            for direction, on, edge in ((1, z + 1 < Z, S - 1), (0, z > 0, S)):
-                cross = z == edge
-                go = cross if across else jnp.logical_not(cross)
-                @pl.when(jnp.logical_and(jnp.logical_and(own_core, on), go))
-                def _():
-                    s_copy(sbuf.at[myslot, h], myslot, h, direction).start()
-
-    own_halves(False)
+            fn(s_copy(k, h, q, False))
+
+    def pass_on(k, h, chunks=range(QX)):
+        for q in chunks:
+            @pl.when(jnp.logical_not(jnp.logical_and(own_core, jnp.logical_and(k == myslot, h == c))))
+            def _():
+                s_copy(k, h, q, True).wait_recv()
+            relay(k, h, q, lambda cp: cp.start())
+
+    inner = z == border
+    outer = z != border
+
+    def pass_at(k, h, on, chunks=range(QX)):
+        @pl.when(on)
+        def _():
+            pass_on(k, h, chunks)
+
+    one, two = jnp.where(inner, far, near), jnp.where(inner, near, far)
 
     def w_copies(d, frm):
         at = pl.ds(row0(c, frm), KR)
@@ -304,13 +323,16 @@
         return (rcopy(wbuf.at[at], wbuf.at[at], f_send.at[d], f_recv.at[d], sib),
                 rcopy(dbuf.at[g], dbuf.at[g], g_send.at[d], g_recv.at[d], sib))
 
-    for step in range(Z - 1, 0, -1):
-        for d in (z + step, z - step):
-            @pl.when(jnp.logical_and(d >= 0, d < Z))
-            def _():
-                for cp in w_copies(d, z):
-                    cp.start()
-    own_halves(True)
+    def send_w(d, on):
+        @pl.when(on)
+        def _():
+            for cp in w_copies(d, z):
+                cp.start()
+
+    @pl.when(ways[0][1])
+    def _():
+        for q in range(QX):
+            i_copy(q, 0).start()
     own_fwd = (
         rcopy(w2.at[z], wbuf.at[pl.ds(row0(c, z), KR)], f_send.at[z], f_recv.at[z], sib),
         rcopy(d2.at[z], dbuf.at[c * Z + z], g_send.at[z], g_recv.at[z], sib),
@@ -318,40 +340,29 @@
     for cp in own_fwd:
         cp.start()
     wbuf[pl.ds(row0(c, z), KR), :] = w2[z]
+
+    @pl.when(own_core)
+    def _():
+        sbuf[myslot, c] = x_ref[...]
+
+    with scope("early"):
+        send_x(c == 0, True)
+        send_x(c == 0, False)
+        send_w(jnp.where(upper, 0, Z - 1), inner)
+        send_w(edge, inner)
+        for step in (3, 1, 2):
+            send_w(jnp.where(upper, z - step, z + step), outer)
+        pass_at(near, 0, inner)
+        send_w(jnp.where(upper, S - 1, S), inner)
+        send_x(jnp.logical_and(c == 1, outer), True)
+
     loads[3].wait()
     at_wo = pl.ds(pl.multiple_of(c * per, per), per)
     wo_copy = rcopy(wo_ref, wobuf.at[at_wo], o_send, o_recv, sib)
     wo_copy.start()
     wobuf[at_wo, :] = wo_ref[...]
-
-    near = jnp.where(upper, S - 1, 0)
     for load in loads[4:]:
         load.wait()
-    gain_in = ng_ref[...]
-
-    def pass_on(k, h):
-        @pl.when(jnp.logical_not(jnp.logical_and(own_core, k == myslot)))
-        def _():
-            s_copy(x_ref, k, h, 0).wait_recv()
-            up_down(k, h, lambda cp: cp.start())
-
-    def norm_in(k, h):
-        v = sbuf[k, h].astype(f32)
-        ms = jnp.mean(v * v, axis=-1, keepdims=True)
-        nbuf[k, h] = (v * lax.rsqrt(ms + epsilon) * gain_in).astype(bf16)
-
-    far = 1 - near
-    for h in range(2):
-        pass_on(near, h)
-        norm_in(near, h)
-    for step in range(1, Z):
-        for d in (z + step, z - step):
-            @pl.when(jnp.logical_and(d >= 0, d < Z))
-            def _():
-                for cp in w_copies(z, d):
-                    cp.wait_recv()
-                for cp in f_copies(d, c):
-                    cp.start()
 
     def pick(ref, width, tail):
         wide = Z * width
@@ -364,6 +375,7 @@
             got = part if got is None else got + part
         return jnp.concatenate([got, tail], axis=1) if tail is not None else got
 
+    gain_in = ng_ref[...]
     hi = lax.Precision.HIGHEST
     taps = pick(cw_ref, per, cw_ref[:, INNER : INNER + NB])
     tbias = pick(cb_ref, per, cb_ref[:, INNER : INNER + NB])
@@ -387,47 +399,27 @@
     triu = (ii <= jj).astype(f32)
     low_lane = lax.broadcasted_iota(jnp.int32, (BLOCK, 128), 1) < HEAD_DIM
     margin = CONV - 1
-    for d in range(Z):
-        for cp in f_copies(d, 1 - c):
-            cp.wait_recv()
-    wo_copy.wait_recv()
-    w_steps = jnp.concatenate([dbuf[g][:, 0:KR].astype(f32) for g in range(2 * Z)], axis=1).astype(bf16)
-
-    def p_copies(k, h):
-        b = 2 * k + c
-        slot = lax.rem(z, S)
-        return (rcopy(pbuf.at[k, h], rpart.at[slot], p_send.at[k, h], p_recv.at[slot], {"dp": b, "seq": h}),
-                rcopy(stbuf.at[k, h], rstat.at[slot], t_send.at[k, h], t_recv.at[slot], {"dp": b, "seq": h}))
-
-    half = rows // 2
-
-    def x_copies(h, frm, q):
-        slot = lax.rem(frm, S)
-        at = pl.ds(q * half, half)
-        big = rcopy(pbuf.at[far, h, at], xpart.at[slot, h, at], q_send.at[h, q], x_recv.at[slot, h, q], {"dp": border})
-        if q > 0:
-            return (big,)
-        return (rcopy(stbuf.at[far, h], xstat.at[slot, h], t_send.at[far, h], y_recv.at[slot, h], {"dp": border}), big)
-
-    def b_copies(h, q):
-        where = {"dp": 2 * far + c, "seq": h}
-        at = pl.ds(q * half, half)
-        big = rcopy(bpart.at[h, at], rpart.at[S, at], b_send.at[h, q], b_recv.at[q], where)
-        if q > 0:
-            return (big,)
-        return (rcopy(bstat.at[h], rstat.at[S], c_send.at[h], t_recv.at[S], where), big)
-
-    def unit(k, h):
+
+    def norm_in(k, h):
+        v = sbuf[k, h].astype(f32)
+        ms = jnp.mean(v * v, axis=-1, keepdims=True)
+        nbuf[k, h] = (v * lax.rsqrt(ms + epsilon) * gain_in).astype(bf16)
+
+    def unit(k, h, hook=None):
         nb = nbuf[k, h]
         if h == 0:
             cbuf[0:8, :] = jnp.zeros((8, CC), f32)
         else:
-            cbuf[0:8, :] = cbuf[rows : rows + 8, :]
+            cbuf[0:8, :] = tails[k]
         cbuf[8 : 8 + rows, :] = jnp.dot(nb, wbuf[...], preferred_element_type=f32).astype(bf16).astype(f32)
+        if h == 0:
+            tails[k] = cbuf[rows : rows + 8, :]
         acc = jnp.broadcast_to(tbias, (rows, CC))
         for t in range(CONV):
             acc = acc + taps[t : t + 1, :] * cbuf[8 - margin + t : 8 - margin + t + rows, :]
         vbuf[...] = (acc / (1.0 + jnp.exp(-acc))).astype(bf16)
+        if hook is not None:
+            hook()
         raw = lax.dot_general(w_steps, nb, (((1,), (1,)), ((), ())), preferred_element_type=f32) + dtb
         dt_t = jnp.maximum(raw, 0.0) + jnp.log1p(jnp.exp(-jnp.abs(raw)))
         cum_t = jnp.dot(-dt_t * rate, triu, precision=hi, preferred_element_type=f32)
@@ -442,7 +434,7 @@
         part = skip_wide * vals
         if h > 0:
             grow = widen(cols[:, 32:48])
-            part = part + grow * jnp.dot(cm.astype(f32), state[...], precision=hi,
+            part = part + grow * jnp.dot(cm.astype(f32), state[k], precision=hi,
                                          preferred_element_type=f32)
         for p in range(VC // 128):
             mix = []
@@ -462,109 +454,191 @@
                                       precision=hi, preferred_element_type=f32)
         if h == 0:
             scaled = (vals * widen(cols[:, 16:32])).astype(bf16)
-            state[...] = lax.dot_general(bm, scaled, (((0,), (0,)), ((), ())), preferred_element_type=f32)
+            state[k] = lax.dot_general(bm, scaled, (((0,), (0,)), ((), ())), preferred_element_type=f32)
+
+    def place(b, h):
+        return {"dp": b, "seq": h}
+
+    def here(h):
+        return jnp.logical_and(own_core, h == c)
+
+    def p_copies(h):
+        slot = lax.rem(z, S)
+        where = place(2 * near + c, h)
+        return (rcopy(stbuf.at[near, h], rstat.at[slot], t_send.at[near, h], t_recv.at[slot], where),
+                *(rcopy(pbuf.at[near, h, band(q, QP)], rpart.at[slot, band(q, QP)], p_send.at[h, q],
+                        p_recv.at[slot, q], where) for q in range(QP)))
+
+    def x_copies(h, q):
+        at = band(q, QP)
+        big = rcopy(pbuf.at[far, h, at], xpart.at[h, at], q_send.at[h, q], x_recv.at[h, q], {"dp": border})
+        if q > 0:
+            return (big,)
+        return (rcopy(stbuf.at[far, h], xstat.at[h], t_send.at[far, h], y_recv.at[h], {"dp": border}), big)
+
+    def b_copies(h, q):
+        where = place(2 * far + c, h)
+        at = band(q, QP)
+        big = rcopy(bpart.at[h, at], rpart.at[S, at], b_send.at[h, q], p_recv.at[S, q], where)
+        if q > 0:
+            return (big,)
+        return (rcopy(bstat.at[h], rstat.at[S], c_send.at[h], t_recv.at[S], where), big)
 
     def send_far(h):
-        @pl.when(z != border)
+        @pl.when(outer)
         def _():
-            for q in range(2):
-                for cp in x_copies(h, z, q):
+            for q in range(QP):
+                for cp in x_copies(h, q):
                     cp.start()
+
+    def send_near(h, now):
+        @pl.when(jnp.logical_and(now, here(h)))
+        def _():
+            rpart[lax.rem(z, S)] = pbuf[near, h]
+            rstat[lax.rem(z, S)] = stbuf[near, h]
+
+        @pl.when(jnp.logical_and(now, jnp.logical_not(here(h))))
+        def _():
+            for cp in p_copies(h):
+                cp.start()
 
     def sum_far(h):
         @pl.when(z == border)
         def _():
-            for q in range(2):
-                r = slice(q * half, (q + 1) * half)
-                total = pbuf[far, h, r].astype(f32)
-                stat = stbuf[far, h]
-                for j in range(S):
-                    frm = jnp.where(upper, S + j, j)
-                    @pl.when(frm != border)
-                    def _():
-                        for cp in x_copies(h, frm, q):
-                            cp.wait_recv()
-                    total = total + jnp.where(frm == border, 0.0, xpart[j, h, r].astype(f32))
-                    stat = stat + jnp.where(frm == border, 0.0, xstat[j, h])
-                bpart[h, r] = total.astype(bf16)
+            for q in range(QP):
+                at = band(q, QP)
+                for cp in x_copies(h, q):
+                    cp.wait_recv()
+                bpart[h, at] = (pbuf[far, h, at].astype(f32) + xpart[h, at].astype(f32)).astype(bf16)
                 if q == 0:
-                    bstat[h] = stat
+                    bstat[h] = stbuf[far, h] + xstat[h]
                 for cp in b_copies(h, q):
                     cp.start()
 
-    def here(k, h):
-        return jnp.logical_and(2 * k + c == z, h == c)
-
-    def send_near(h, now):
-        @pl.when(jnp.logical_and(now, here(near, h)))
-        def _():
-            rpart[lax.rem(z, S)] = pbuf[near, h]
-            rstat[lax.rem(z, S)] = stbuf[near, h]
-
-        @pl.when(jnp.logical_and(now, jnp.logical_not(here(near, h))))
-        def _():
-            for cp in p_copies(near, h):
-                cp.start()
-
+    with scope("passf0i"):
+        pass_at(far, 0, inner)
+    send_x(jnp.logical_and(c == 1, inner), True)
+    for step in range(1, Z):
+        for d in (z + step, z - step):
+            @pl.when(jnp.logical_and(d >= 0, d < Z))
+            def _():
+                with scope(f"wrecv{step}"):
+                    for cp in w_copies(z, d):
+                        cp.wait_recv()
+                for cp in f_copies(d, c):
+                    cp.start()
+    with scope("passn1i"):
+        pass_at(near, 1, inner)
+    with scope("fwait"):
+        for d in range(Z):
+            for cp in f_copies(d, 1 - c):
+                cp.wait_recv()
+        wo_copy.wait_recv()
+    w_steps = jnp.concatenate([dbuf[g][:, 0:KR].astype(f32) for g in range(2 * Z)], axis=1).astype(bf16)
+
+    with scope("passf1h"):
+        None
+    with scope("passn0"):
+        pass_at(near, 0, outer)
+    with scope("unit0"):
+        norm_in(one, 0)
+        unit(one, 0, lambda: pass_at(far, 1, inner, (0,)))
+    send_near(0, outer)
+    with scope("passf1i"):
+        pass_at(far, 1, inner, (1,))
+    with scope("passf0"):
+        pass_at(far, 0, outer)
+    with scope("unit1"):
+        norm_in(two, 0)
+        unit(two, 0, lambda: pass_at(far, 1, inner, (2,)))
+    send_far(0)
+    with scope("passf1j"):
+        pass_at(far, 1, inner, (3,))
+    send_x(jnp.logical_and(c == 1, inner), False)
+    with scope("passf1"):
+        pass_at(far, 1, outer)
+    with scope("unit2"):
+        norm_in(two, 1)
+        unit(two, 1)
+    send_far(1)
+    with scope("sumf0"):
+        sum_far(0)
+    with scope("passn1"):
+        pass_at(near, 1, outer)
+    with scope("unit3"):
+        norm_in(one, 1)
+        unit(one, 1)
     for h in range(2):
-        unit(near, h)
-        send_near(h, z != border)
-    for h in range(2):
-        pass_on(far, h)
-        norm_in(far, h)
-        unit(far, h)
-        send_far(h)
-    for h in range(2):
-        send_near(h, z == border)
-    for h in range(2):
-        sum_far(h)
-
-    total = jnp.zeros((rows, D), f32)
-    stat = jnp.zeros((8, rows), f32)
-    for j in range(S + 1):
-        mine = jnp.logical_and(own_core, lax.rem(z, S) == j) if j < S else False
-        @pl.when(jnp.logical_not(mine))
-        def _():
-            if j == S:
-                for q in range(2):
-                    at = pl.ds(q * half, half)
-                    rcopy(pbuf.at[0, 0, at], rpart.at[S, at], b_send.at[0, q], b_recv.at[q], sib).wait_recv()
-            else:
-                rcopy(pbuf.at[0, 0], rpart.at[j], p_send.at[0, 0], p_recv.at[j], sib).wait_recv()
-            rcopy(stbuf.at[0, 0], rstat.at[j], t_send.at[0, 0], t_recv.at[j], sib).wait_recv()
-        total = total + rpart[j].astype(f32)
-        stat = stat + rstat[j]
-    scale = lax.rsqrt(stat * (1.0 / INNER) + epsilon).T[:, 0:1]
-    obuf[...] = (x_ref[...].astype(f32) + total * scale).astype(bf16)
-    last_copy = rcopy(obuf, out_ref, e_send, e_recv, {"section": nxt})
-    last_copy.start()
-
-    @pl.when(jnp.logical_not(own_core))
-    def _():
-        half_out.wait_send()
-    for cp in (*own_fwd, wo_copy):
-        cp.wait_send()
-    for d in range(Z):
-        @pl.when(d != z)
-        def _():
-            for cp in (*w_copies(d, z), *f_copies(d, c)):
-                cp.wait_send()
-    for h in range(2):
-        for k in range(S):
-            up_down(k, h, lambda cp: cp.wait_send())
-        @pl.when(z != border)
-        def _():
-            for cp in (*x_copies(h, z, 0), *x_copies(h, z, 1)):
-                cp.wait_send()
-        @pl.when(z == border)
-        def _():
-            for cp in (*b_copies(h, 0), *b_copies(h, 1)):
-                cp.wait_send()
-        @pl.when(jnp.logical_not(here(near, h)))
-        def _():
-            for cp in p_copies(near, h):
-                cp.wait_send()
-    last_copy.wait()
+        send_near(h, inner)
+    send_near(1, outer)
+    with scope("sumf1"):
+        sum_far(1)
+    def r_copies(j, q):
+        at = band(q, QP)
+        big = rcopy(pbuf.at[0, 0, at], rpart.at[j, at], p_send.at[0, q], p_recv.at[j, q], sib)
+        if q > 0:
+            return (big,)
+        return (rcopy(stbuf.at[0, 0], rstat.at[j], t_send.at[0, 0], t_recv.at[j], sib), big)
+
+    def e_copy(q):
+        at = band(q, QP)
+        return rcopy(obuf.at[at], out_ref.at[at], e_send.at[q], e_recv.at[q], {"section": nxt})
+
+    scale = None
+    for q in range(QP):
+        at = band(q, QP)
+        with scope(f"rwait{q}"):
+            for j in range(S + 1):
+                mine = jnp.logical_and(own_core, lax.rem(z, S) == j) if j < S else False
+                @pl.when(jnp.logical_not(mine))
+                def _():
+                    for cp in r_copies(j, q):
+                        cp.wait_recv()
+        if q == 0:
+            stat = rstat[0]
+            for j in range(1, S + 1):
+                stat = stat + rstat[j]
+            scale = lax.rsqrt(stat * (1.0 / INNER) + epsilon).T[:, 0:1]
+        total = rpart[0, at].astype(f32)
+        for j in range(1, S + 1):
+            total = total + rpart[j, at].astype(f32)
+        size = rows // QP
+        obuf[at, :] = (x_ref[at].astype(f32) + total * scale[q * size : (q + 1) * size]).astype(bf16)
+        e_copy(q).start()
+
+    with scope("sends"):
+        for q in range(QX):
+            for way, on in ways:
+                @pl.when(on)
+                def _():
+                    i_copy(q, way).wait_send()
+        for cp in (*own_fwd, wo_copy):
+            cp.wait_send()
+        for d in range(Z):
+            @pl.when(d != z)
+            def _():
+                for cp in (*w_copies(d, z), *f_copies(d, c)):
+                    cp.wait_send()
+        for h in range(2):
+            for q in range(QX):
+                for k in range(S):
+                    relay(k, h, q, lambda cp: cp.wait_send())
+            for q in range(QP):
+                @pl.when(z != border)
+                def _():
+                    for cp in x_copies(h, q):
+                        cp.wait_send()
+                @pl.when(z == border)
+                def _():
+                    for cp in b_copies(h, q):
+                        cp.wait_send()
+            @pl.when(jnp.logical_not(here(h)))
+            def _():
+                for cp in p_copies(h):
+                    cp.wait_send()
+    with scope("last"):
+        for q in range(QP):
+            e_copy(q).wait()
 
 
 def fused(
@@ -598,22 +672,26 @@
             V((Z, 16, lanes), bf16), V((2 * Z, 16, lanes), bf16),
             V((VC, D), bf16),
             V((S, 2, rows, D), bf16), V((S, 2, rows, D), bf16),
-            V((8 + rows, CC), f32), V((rows, CC), bf16), V((rows, VC), f32), V((STATE, VC), f32),
+            V((8 + rows, CC), f32), V((S, 8, CC), f32), V((rows, CC), bf16), V((rows, VC), f32),
+            V((S, STATE, VC), f32),
             V((S, 2, rows, D), bf16), V((S, 2, 8, rows), f32),
-            V((S, 2, rows, D), bf16), V((S, 2, 8, rows), f32),
+            V((2, rows, D), bf16), V((2, 8, rows), f32),
             V((2, rows, D), bf16), V((2, 8, rows), f32),
             V((S + 1, rows, D), bf16), V((S + 1, 8, rows), f32),
             V((rows, D), bf16),
             dma((11,)), dma((Z,)), dma((Z,)), dma((Z,)), dma((Z,)), dma((Z,)), dma((Z,)), dma((Z,)),
-            dma((Z,)), dma, dma, dma((S, 2, 2)), dma((S, 2)), dma, dma((S, 2)), dma((S + 1,)),
-            dma((S, 2)), dma((S + 1,)), dma((S, 2, 2)), dma((S, 2)), dma((2, 2)), dma((2,)), dma((2, 2)), dma((2,)), dma, dma,
+            dma((Z,)), dma, dma,
+            dma((3, QX)), dma((S, 2, QX)), dma((S, 2, QX)), dma((QP,)), dma((QP,)), dma((2, QP)), dma((S + 1, QP)),
+            dma((S, 2)), dma((S + 1,)),
+            dma((2, QP)), dma((2, QP)), dma((2,)), dma((2, QP)), dma((2,)),
         ],
         compiler_params=pltpu.CompilerParams(
-            collective_id=0, has_side_effects=True, vmem_limit_bytes=67043328
+            collective_id=0, has_side_effects=True, vmem_limit_bytes=50 * 1024 * 1024
         ),
     )(
-        stream[0, 0], norm_gain, w_xbc[0], jnp.swapaxes(w_dt, 1, 2)[0], conv_weight[0], conv_bias,
-        dt_bias, decay_rate, skip_weight, inner_gain, w_out[0],
+        *(pltpu.with_memory_space_constraint(a, pltpu.HBM) for a in (
+            stream[0, 0], norm_gain, w_xbc[0], jnp.swapaxes(w_dt, 1, 2)[0], conv_weight[0], conv_bias,
+            dt_bias, decay_rate, skip_weight, inner_gain, w_out[0]))
     )
     return out[None, None]
 

time: 81.7 us -> 71.9 us (0.88)
  Pallas kernels: 79 us -> 70.6 us
  local copies, waits for them, and re-layouts: 1.72 us -> 0.73 us
    pallas_call x1, Pallas kernels: 79 us -> 70.6 us  [fused(): pl.pallas_call(functools.partial(section_kernel, Z), out_shape=jax.ShapeD...]
    unnamed x1, local copies, waits for them, and re-layouts: 1.72 us -> 0.73 us
where the time goes in v2:
time: 71.9 us; the launch traced here: 71.3 us
  Pallas kernels  70.6 us (98%)
  local copies, waits for them, and re-layouts  0.73 us (1%)
    pallas_call x1, Pallas kernels, fused(): pl.pallas_call(functools.partial(section_kernel, Z), out_shape=jax.ShapeD...  70.6 us

profile of v2, /device:TPU:1, one launch (start us, length us, event | category | flops | bytes accessed | tf_op | source)
XLA Modules:
  0.0 71.3 jit_solution(2502816006439765973)
XLA Ops:
  0.0 70.6 %shard_map.109 = bf16[128,1280]{1,0:T(8,128)(2,1)S(1)} custom-call(bf16[128,1280]{1,0:T(8,128)(2,1)} %bitcast.11, f32[1,1280]{1,0:T(1,128)} %ng_hbm.1, bf16[160,2688]{1,0:T(8,128)(2,1)} %bitcast.9, bf16[40,160]{1,0:T(8,128)(2,1)} %bitcast.13, f32[4,2688]{1,0:T(4,128)} %bitcast.12, f32[1,2688]{1,0:T(1,128)} %cb_hbm.1, f32[1,40]{1,0:T(1,128)} %db_hbm.1, ...), custom_call_target="tpu_custom_call" | custom-call | tf_op jit(solution)/shard_map/pallas_call | solution.py:661
  70.6 0.7 %copy.13 = bf16[1,1,128,1280]{3,2,1,0:T(8,128)(2,1)} copy(bf16[1,1,128,1280]{3,2,1,0:T(8,128)(2,1)S(1)} %bitcast.8) | data formatting | bytes 655360

commit v3 on v2

--- a/solution.py
+++ b/solution.py
@@ -183,10 +183,10 @@
     out_ref,
     x_ref, ng_ref, w_ref, wd_ref, cw_ref, cb_ref, db_ref, dr_ref, sk_ref, ig_ref, wo_ref, w2,
     wbuf, d2, dbuf, wobuf, sbuf, nbuf, cbuf, tails, vbuf, ybuf, state,
-    pbuf, stbuf, xpart, xstat, bpart, bstat, rpart, rstat, obuf,
+    pbuf, stbuf, xpart, xstat, bpart, bstat, kpart, kstat, jpart, jstat, rpart, rstat, obuf,
     l_sem, w_send, w_recv, d_send, d_recv, f_send, f_recv, g_send, g_recv, o_send, o_recv,
     i_send, s_send, s_recv, e_send, e_recv, p_send, p_recv, t_send, t_recv,
-    q_send, x_recv, y_recv, b_send, c_send,
+    q_send, x_recv, y_recv, b_send, c_send, k_recv, kt_recv, j_send, jt_send,
 ):
     z = lax.axis_index("dp")
     c = lax.axis_index("seq")
@@ -267,22 +267,29 @@
 
     def i_copy(q, way):
         where = sib if way == 0 else {"dp": z + (1 if way == 1 else -1), "seq": core}
-        at = band(q, QX)
-        return rcopy(x_ref.at[at], sbuf.at[myslot, c, at], i_send.at[way, q], s_recv.at[myslot, c, q], where)
-
+        at = band(0, 1) if q is None else band(q, QX)
+        q = q or 0
+        return rcopy(x_ref.at[at], sbuf.at[myslot, c, at], i_send.at[way], s_recv.at[myslot, c, q], where)
+
+    inner, outer = z == border, z != border
     ways = ((0, jnp.logical_not(own_core)), (1, z + 1 < Z), (2, z > 0))
+    summer = jnp.logical_and(inner, own_core)
+    joiner = jnp.logical_and(inner, jnp.logical_not(own_core))
 
     def send_x(on, inward):
         for way, there in ways[1:]:
             towards = jnp.logical_xor(upper, way == 1)
+            if inward:
+                there = jnp.logical_and(there, outer)
             @pl.when(jnp.logical_and(jnp.logical_and(on, there), towards if inward else jnp.logical_not(towards)))
             def _():
                 for q in range(QX):
                     i_copy(q, way).start()
 
     def s_copy(k, h, q, up):
-        at = band(q, QX)
-        return rcopy(sbuf.at[k, h, at], sbuf.at[k, h, at], s_send.at[k, h, q], s_recv.at[k, h, q],
+        at = band(0, 1) if q is None else band(q, QX)
+        q = q or 0
+        return rcopy(sbuf.at[k, h, at], sbuf.at[k, h, at], s_send.at[k, h], s_recv.at[k, h, q],
                      {"dp": z + (1 if up else -1)})
 
     def relay(k, h, q, fn):
@@ -293,6 +300,13 @@
         @pl.when(jnp.logical_and(z < b, z > 0))
         def _():
             fn(s_copy(k, h, q, False))
+
+    def own_on(h, q, fn):
+        at = band(0, 1) if q is None else band(q, QX)
+        @pl.when(summer)
+        def _():
+            fn(rcopy(sbuf.at[near, h, at], sbuf.at[near, h, at], s_send.at[near, h],
+                     s_recv.at[near, h, q or 0], {"dp": jnp.where(upper, z - 1, z + 1)}))
 
     def pass_on(k, h, chunks=range(QX)):
         for q in chunks:
@@ -301,8 +315,6 @@
                 s_copy(k, h, q, True).wait_recv()
             relay(k, h, q, lambda cp: cp.start())
 
-    inner = z == border
-    outer = z != border
 
     def pass_at(k, h, on, chunks=range(QX)):
         @pl.when(on)
@@ -314,45 +326,57 @@
     def w_copies(d, frm):
         at = pl.ds(row0(c, frm), KR)
         g = c * Z + frm
-        return (rcopy(w2.at[d], wbuf.at[at], w_send.at[d], w_recv.at[frm], {"dp": d}),
-                rcopy(d2.at[d], dbuf.at[g], d_send.at[d], d_recv.at[frm], {"dp": d}))
+        return (rcopy(w2.at[d], wbuf.at[at], w_send, w_recv.at[frm], {"dp": d}),
+                rcopy(d2.at[d], dbuf.at[g], d_send, d_recv.at[frm], {"dp": d}))
 
     def f_copies(d, core):
         at = pl.ds(row0(core, d), KR)
         g = core * Z + d
-        return (rcopy(wbuf.at[at], wbuf.at[at], f_send.at[d], f_recv.at[d], sib),
-                rcopy(dbuf.at[g], dbuf.at[g], g_send.at[d], g_recv.at[d], sib))
+        return (rcopy(wbuf.at[at], wbuf.at[at], f_send, f_recv, sib),
+                rcopy(dbuf.at[g], dbuf.at[g], g_send, g_recv, sib))
+
+    def forwards():
+        half = pl.ds(0, Z * KR)
+        return (rcopy(wbuf.at[half], wbuf.at[half], f_send, f_recv, sib),
+                rcopy(dbuf.at[pl.ds(0, Z)], dbuf.at[pl.ds(0, Z)], g_send, g_recv, sib))
 
     def send_w(d, on):
         @pl.when(on)
         def _():
             for cp in w_copies(d, z):
                 cp.start()
-
-    @pl.when(ways[0][1])
-    def _():
-        for q in range(QX):
-            i_copy(q, 0).start()
-    own_fwd = (
-        rcopy(w2.at[z], wbuf.at[pl.ds(row0(c, z), KR)], f_send.at[z], f_recv.at[z], sib),
-        rcopy(d2.at[z], dbuf.at[c * Z + z], g_send.at[z], g_recv.at[z], sib),
-    )
-    for cp in own_fwd:
-        cp.start()
-    wbuf[pl.ds(row0(c, z), KR), :] = w2[z]
 
     @pl.when(own_core)
     def _():
         sbuf[myslot, c] = x_ref[...]
 
     with scope("early"):
+        @pl.when(ways[0][1])
+        def _():
+            for q in range(QX):
+                i_copy(q, 0).start()
         send_x(c == 0, True)
         send_x(c == 0, False)
+        @pl.when(c == 0)
+        def _():
+            for q in range(QX):
+                own_on(0, q, lambda cp: cp.start())
         send_w(jnp.where(upper, 0, Z - 1), inner)
         send_w(edge, inner)
         for step in (3, 1, 2):
             send_w(jnp.where(upper, z - step, z + step), outer)
+        own_fwd = (
+            rcopy(w2.at[z], wbuf.at[pl.ds(row0(c, z), KR)], f_send, f_recv, sib),
+            rcopy(d2.at[z], dbuf.at[c * Z + z], g_send, g_recv, sib),
+        )
+        for cp in own_fwd:
+            cp.start()
+        wbuf[pl.ds(row0(c, z), KR), :] = w2[z]
         pass_at(near, 0, inner)
+        @pl.when(c == 1)
+        def _():
+            for q in range(QX):
+                own_on(0, q, lambda cp: cp.start())
         send_w(jnp.where(upper, S - 1, S), inner)
         send_x(jnp.logical_and(c == 1, outer), True)
 
@@ -462,27 +486,54 @@
     def here(h):
         return jnp.logical_and(own_core, h == c)
 
-    def p_copies(h):
+    def p_copies(h, whole=False):
         slot = lax.rem(z, S)
         where = place(2 * near + c, h)
+        parts = 1 if whole else QP
         return (rcopy(stbuf.at[near, h], rstat.at[slot], t_send.at[near, h], t_recv.at[slot], where),
-                *(rcopy(pbuf.at[near, h, band(q, QP)], rpart.at[slot, band(q, QP)], p_send.at[h, q],
-                        p_recv.at[slot, q], where) for q in range(QP)))
+                *(rcopy(pbuf.at[near, h, band(q, parts)], rpart.at[slot, band(q, parts)], p_send.at[h],
+                        p_recv.at[slot, q], where) for q in range(parts)))
 
     def x_copies(h, q):
-        at = band(q, QP)
-        big = rcopy(pbuf.at[far, h, at], xpart.at[h, at], q_send.at[h, q], x_recv.at[h, q], {"dp": border})
+        at, q = (band(0, 1), 0) if q is None else (band(q, QP), q)
+        big = rcopy(pbuf.at[far, h, at], xpart.at[h, at], q_send.at[h], x_recv.at[h, q], {"dp": border})
         if q > 0:
             return (big,)
         return (rcopy(stbuf.at[far, h], xstat.at[h], t_send.at[far, h], y_recv.at[h], {"dp": border}), big)
 
-    def b_copies(h, q):
-        where = place(2 * far + c, h)
-        at = band(q, QP)
-        big = rcopy(bpart.at[h, at], rpart.at[S, at], b_send.at[h, q], p_recv.at[S, q], where)
+    def b_copies(h, q, join):
+        at, q = (band(0, 1), 0) if q is None else (band(q, QP), q)
+        if join:
+            where = {"dp": Z - 1 - z}
+            big, small = (kpart.at[h, at], k_recv.at[h, q]), (kstat.at[h], kt_recv.at[h])
+        else:
+            where = place(2 * far + c, h)
+            big, small = (rpart.at[S, at], p_recv.at[S, q]), (rstat.at[S], t_recv.at[S])
+        big = rcopy(bpart.at[h, at], big[0], b_send.at[h], big[1], where)
         if q > 0:
             return (big,)
-        return (rcopy(bstat.at[h], rstat.at[S], c_send.at[h], t_recv.at[S], where), big)
+        return (rcopy(bstat.at[h], small[0], c_send.at[h], small[1], where), big)
+
+    def j_copies(h, q):
+        where = place(edge, h)
+        at, q = (band(0, 1), 0) if q is None else (band(q, QP), q)
+        big = rcopy(jpart.at[h, at], rpart.at[S, at], j_send.at[h], p_recv.at[S, q], where)
+        if q > 0:
+            return (big,)
+        return (rcopy(jstat.at[h], rstat.at[S], jt_send.at[h], t_recv.at[S], where), big)
+
+    def join_near(h, chunks=range(QP)):
+        @pl.when(joiner)
+        def _():
+            for q in chunks:
+                at = band(q, QP)
+                for cp in b_copies(h, q, True):
+                    cp.wait_recv()
+                jpart[h, at] = (pbuf[near, h, at].astype(f32) + kpart[h, at].astype(f32)).astype(bf16)
+                if q == 0:
+                    jstat[h] = stbuf[near, h] + kstat[h]
+                for cp in j_copies(h, q):
+                    cp.start()
 
     def send_far(h):
         @pl.when(outer)
@@ -497,27 +548,31 @@
             rpart[lax.rem(z, S)] = pbuf[near, h]
             rstat[lax.rem(z, S)] = stbuf[near, h]
 
-        @pl.when(jnp.logical_and(now, jnp.logical_not(here(h))))
+        @pl.when(jnp.logical_and(jnp.logical_and(now, jnp.logical_not(joiner)), jnp.logical_not(here(h))))
         def _():
             for cp in p_copies(h):
                 cp.start()
 
-    def sum_far(h):
-        @pl.when(z == border)
-        def _():
-            for q in range(QP):
+    def sum_far(h, chunks=range(QP), on=True):
+        @pl.when(jnp.logical_and(inner, on))
+        def _():
+            for q in chunks:
                 at = band(q, QP)
                 for cp in x_copies(h, q):
                     cp.wait_recv()
                 bpart[h, at] = (pbuf[far, h, at].astype(f32) + xpart[h, at].astype(f32)).astype(bf16)
                 if q == 0:
                     bstat[h] = stbuf[far, h] + xstat[h]
-                for cp in b_copies(h, q):
-                    cp.start()
+                for on, join in ((own_core, True), (jnp.logical_not(own_core), False)):
+                    @pl.when(on)
+                    def _():
+                        for cp in b_copies(h, q, join):
+                            cp.start()
 
     with scope("passf0i"):
         pass_at(far, 0, inner)
-    send_x(jnp.logical_and(c == 1, inner), True)
+    with scope('passn1i'):
+        pass_at(near, 1, joiner)
     for step in range(1, Z):
         for d in (z + step, z - step):
             @pl.when(jnp.logical_and(d >= 0, d < Z))
@@ -527,118 +582,139 @@
                         cp.wait_recv()
                 for cp in f_copies(d, c):
                     cp.start()
-    with scope("passn1i"):
-        pass_at(near, 1, inner)
     with scope("fwait"):
-        for d in range(Z):
-            for cp in f_copies(d, 1 - c):
-                cp.wait_recv()
+        for cp in forwards():
+            cp.wait_recv()
         wo_copy.wait_recv()
     w_steps = jnp.concatenate([dbuf[g][:, 0:KR].astype(f32) for g in range(2 * Z)], axis=1).astype(bf16)
 
+    def r_copies(j, q):
+        at = band(q, QP)
+        big = rcopy(pbuf.at[0, 0, at], rpart.at[j, at], p_send.at[0], p_recv.at[j, q], sib)
+        if q > 0:
+            return (big,)
+        return (rcopy(stbuf.at[0, 0], rstat.at[j], t_send.at[0, 0], t_recv.at[j], sib), big)
+
+    def e_copy(q, parts=QP):
+        at = band(q, parts)
+        return rcopy(obuf.at[at], out_ref.at[at], e_send, e_recv, {"section": nxt})
+
+    def finish():
+        scale = None
+        for q in range(QP):
+            at = band(q, QP)
+            with scope(f"rwait{q}"):
+                for j in range(S + 1):
+                    own = lax.rem(z, S) == j
+                    take = jnp.logical_or(jnp.logical_and(own, jnp.logical_not(own_core)),
+                                          jnp.logical_and(inner, jnp.logical_not(own))) if j < S else True
+                    @pl.when(take)
+                    def _():
+                        for cp in r_copies(j, q):
+                            cp.wait_recv()
+            if q == 0:
+                stat = rstat[S]
+                for j in range(S):
+                    stat = stat + jnp.where(jnp.logical_or(inner, lax.rem(z, S) == j), rstat[j], 0.0)
+                scale = lax.rsqrt(stat * (1.0 / INNER) + epsilon).T[:, 0:1]
+            total = rpart[S, at].astype(f32)
+            for j in range(S):
+                part = rpart[j, at].astype(f32)
+                total = total + jnp.where(jnp.logical_or(inner, lax.rem(z, S) == j), part, 0.0)
+            size = rows // QP
+            obuf[at, :] = (x_ref[at].astype(f32) + total * scale[q * size : (q + 1) * size]).astype(bf16)
+            e_copy(q).start()
+
+    with scope('own1'):
+        pass_at(near, 1, summer)
+        for q in range(QX):
+            own_on(1, q, lambda cp: cp.start())
+
     with scope("passf1h"):
-        None
+        pass_at(far, 1, summer)
     with scope("passn0"):
         pass_at(near, 0, outer)
     with scope("unit0"):
         norm_in(one, 0)
-        unit(one, 0, lambda: pass_at(far, 1, inner, (0,)))
-    send_near(0, outer)
+        unit(one, 0, lambda: pass_at(far, 1, joiner, (0,)))
     with scope("passf1i"):
-        pass_at(far, 1, inner, (1,))
+        pass_at(far, 1, joiner, (1,))
+    send_x(jnp.logical_and(c == 1, inner), False)
     with scope("passf0"):
         pass_at(far, 0, outer)
     with scope("unit1"):
         norm_in(two, 0)
-        unit(two, 0, lambda: pass_at(far, 1, inner, (2,)))
+        unit(two, 0, lambda: pass_at(far, 1, joiner, (2,)))
     send_far(0)
+    send_near(0, outer)
     with scope("passf1j"):
-        pass_at(far, 1, inner, (3,))
-    send_x(jnp.logical_and(c == 1, inner), False)
+        pass_at(far, 1, joiner, (3,))
+    with scope("sumf0"):
+        sum_far(0)
     with scope("passf1"):
         pass_at(far, 1, outer)
     with scope("unit2"):
-        norm_in(two, 1)
-        unit(two, 1)
+        norm_in(far, 1)
+        unit(far, 1)
     send_far(1)
-    with scope("sumf0"):
-        sum_far(0)
+    with scope("sums1"):
+        sum_far(1, on=summer)
+    send_near(0, inner)
     with scope("passn1"):
         pass_at(near, 1, outer)
     with scope("unit3"):
-        norm_in(one, 1)
-        unit(one, 1)
-    for h in range(2):
-        send_near(h, inner)
+        norm_in(near, 1)
+        unit(near, 1)
+    send_near(1, inner)
     send_near(1, outer)
+    with scope("join0"):
+        join_near(0)
+    with scope("fin0"):
+        @pl.when(c == 0)
+        def _():
+            finish()
+    with scope("join1"):
+        join_near(1)
     with scope("sumf1"):
-        sum_far(1)
-    def r_copies(j, q):
-        at = band(q, QP)
-        big = rcopy(pbuf.at[0, 0, at], rpart.at[j, at], p_send.at[0, q], p_recv.at[j, q], sib)
-        if q > 0:
-            return (big,)
-        return (rcopy(stbuf.at[0, 0], rstat.at[j], t_send.at[0, 0], t_recv.at[j], sib), big)
-
-    def e_copy(q):
-        at = band(q, QP)
-        return rcopy(obuf.at[at], out_ref.at[at], e_send.at[q], e_recv.at[q], {"section": nxt})
-
-    scale = None
-    for q in range(QP):
-        at = band(q, QP)
-        with scope(f"rwait{q}"):
-            for j in range(S + 1):
-                mine = jnp.logical_and(own_core, lax.rem(z, S) == j) if j < S else False
-                @pl.when(jnp.logical_not(mine))
-                def _():
-                    for cp in r_copies(j, q):
-                        cp.wait_recv()
-        if q == 0:
-            stat = rstat[0]
-            for j in range(1, S + 1):
-                stat = stat + rstat[j]
-            scale = lax.rsqrt(stat * (1.0 / INNER) + epsilon).T[:, 0:1]
-        total = rpart[0, at].astype(f32)
-        for j in range(1, S + 1):
-            total = total + rpart[j, at].astype(f32)
-        size = rows // QP
-        obuf[at, :] = (x_ref[at].astype(f32) + total * scale[q * size : (q + 1) * size]).astype(bf16)
-        e_copy(q).start()
-
+        sum_far(1, on=joiner)
+    with scope("fin1"):
+        @pl.when(c == 1)
+        def _():
+            finish()
     with scope("sends"):
-        for q in range(QX):
-            for way, on in ways:
-                @pl.when(on)
-                def _():
-                    i_copy(q, way).wait_send()
-        for cp in (*own_fwd, wo_copy):
+        for way, on in ways:
+            on = on if way == 0 else jnp.logical_and(on, jnp.logical_or(outer, jnp.logical_xor(upper, way == 2)))
+            @pl.when(on)
+            def _():
+                i_copy(None, way).wait_send()
+        wo_copy.wait_send()
+        for cp in forwards():
             cp.wait_send()
-        for d in range(Z):
-            @pl.when(d != z)
+        others = pl.ds(0, Z - 1)
+        rcopy(w2.at[others], w2.at[others], w_send, w_recv.at[0], sib).wait_send()
+        rcopy(d2.at[others], d2.at[others], d_send, d_recv.at[0], sib).wait_send()
+        for h in range(2):
+            for k in range(S):
+                relay(k, h, None, lambda cp: cp.wait_send())
+            own_on(h, None, lambda cp: cp.wait_send())
+            @pl.when(outer)
             def _():
-                for cp in (*w_copies(d, z), *f_copies(d, c)):
+                for cp in x_copies(h, None):
                     cp.wait_send()
-        for h in range(2):
-            for q in range(QX):
-                for k in range(S):
-                    relay(k, h, q, lambda cp: cp.wait_send())
-            for q in range(QP):
-                @pl.when(z != border)
-                def _():
-                    for cp in x_copies(h, q):
-                        cp.wait_send()
-                @pl.when(z == border)
-                def _():
-                    for cp in b_copies(h, q):
-                        cp.wait_send()
-            @pl.when(jnp.logical_not(here(h)))
+            @pl.when(inner)
             def _():
-                for cp in p_copies(h):
+                for cp in b_copies(h, None, True):
+                    cp.wait_send()
+            @pl.when(joiner)
+            def _():
+                for cp in j_copies(h, None):
+                    cp.wait_send()
+            @pl.when(jnp.logical_not(jnp.logical_or(joiner, here(h))))
+            def _():
+                for cp in p_copies(h, True):
                     cp.wait_send()
     with scope("last"):
-        for q in range(QP):
-            e_copy(q).wait()
+        e_copy(0, 1).wait()
 
 
 def fused(
@@ -662,7 +738,7 @@
         functools.partial(section_kernel, Z),
         out_shape=jax.ShapeDtypeStruct((rows, D), bf16),
         in_specs=[far] * 11,
-        out_specs=held,
+        out_specs=pl.BlockSpec(memory_space=pl.ANY),
         scratch_shapes=[
             V((rows, D), bf16), V(norm_gain.shape, f32), V(w_xbc.shape[1:], bf16),
             V((HEADS, KR), bf16), V(conv_weight.shape[1:], f32), V(conv_bias.shape, f32),
@@ -677,13 +753,15 @@
             V((S, 2, rows, D), bf16), V((S, 2, 8, rows), f32),
             V((2, rows, D), bf16), V((2, 8, rows), f32),
             V((2, rows, D), bf16), V((2, 8, rows), f32),
+            V((2, rows, D), bf16), V((2, 8, rows), f32),
+            V((2, rows, D), bf16), V((2, 8, rows), f32),
             V((S + 1, rows, D), bf16), V((S + 1, 8, rows), f32),
             V((rows, D), bf16),
-            dma((11,)), dma((Z,)), dma((Z,)), dma((Z,)), dma((Z,)), dma((Z,)), dma((Z,)), dma((Z,)),
-            dma((Z,)), dma, dma,
-            dma((3, QX)), dma((S, 2, QX)), dma((S, 2, QX)), dma((QP,)), dma((QP,)), dma((2, QP)), dma((S + 1, QP)),
+            dma((11,)), dma, dma((Z,)), dma, dma((Z,)), dma, dma, dma, dma, dma, dma,
+            dma((3,)), dma((S, 2)), dma((S, 2, QX)), dma, dma, dma((2,)), dma((S + 1, QP)),
             dma((S, 2)), dma((S + 1,)),
-            dma((2, QP)), dma((2, QP)), dma((2,)), dma((2, QP)), dma((2,)),
+            dma((2,)), dma((2, QP)), dma((2,)), dma((2,)), dma((2,)), dma((2, QP)), dma((2,)),
+            dma((2,)), dma((2,)),
         ],
         compiler_params=pltpu.CompilerParams(
             collective_id=0, has_side_effects=True, vmem_limit_bytes=50 * 1024 * 1024

time: 71.9 us -> 69 us (0.960)
  Pallas kernels: 70.6 us -> 67.4 us
    pallas_call x1, Pallas kernels: 70.6 us -> 67.4 us  [fused(): pl.pallas_call(functools.partial(section_kernel, Z), out_shape=jax.ShapeD...]
where the time goes in v3:
time: 69 us; the launch traced here: 68.1 us
  Pallas kernels  67.4 us (98%)
  local copies, waits for them, and re-layouts  0.73 us (1%)
    pallas_call x1, Pallas kernels, fused(): pl.pallas_call(functools.partial(section_kernel, Z), out_shape=jax.ShapeD...  67.4 us

profile of v3, /device:TPU:1, one launch (start us, length us, event | category | flops | bytes accessed | tf_op | source)
XLA Modules:
  0.0 68.1 jit_solution(1871512759838414245)
XLA Ops:
  0.0 67.4 %shard_map.109 = bf16[128,1280]{1,0:T(8,128)(2,1)S(1)} custom-call(bf16[128,1280]{1,0:T(8,128)(2,1)} %bitcast.11, f32[1,1280]{1,0:T(1,128)} %ng_hbm.1, bf16[160,2688]{1,0:T(8,128)(2,1)} %bitcast.9, bf16[40,160]{1,0:T(8,128)(2,1)} %bitcast.13, f32[4,2688]{1,0:T(4,128)} %bitcast.12, f32[1,2688]{1,0:T(1,128)} %cb_hbm.1, f32[1,40]{1,0:T(1,128)} %db_hbm.1, ...), custom_call_target="tpu_custom_call" | custom-call | tf_op jit(solution)/shard_map/pallas_call | solution.py:737
  67.4 0.7 %copy.13 = bf16[1,1,128,1280]{3,2,1,0:T(8,128)(2,1)} copy(bf16[1,1,128,1280]{3,2,1,0:T(8,128)(2,1)S(1)} %bitcast.8) | data formatting | bytes 655360

commit v4 on v3

--- a/solution.py
+++ b/solution.py
@@ -400,7 +400,6 @@
         return jnp.concatenate([got, tail], axis=1) if tail is not None else got
 
     gain_in = ng_ref[...]
-    hi = lax.Precision.HIGHEST
     taps = pick(cw_ref, per, cw_ref[:, INNER : INNER + NB])
     tbias = pick(cb_ref, per, cb_ref[:, INNER : INNER + NB])
     hz = jnp.zeros((1, 128 - 2 * hper), f32)
@@ -410,17 +409,22 @@
     heads_t = heads.T[0:16]
     dtb, rate = heads_t[:, 0:1], heads_t[:, 1:2]
     gain_out = pick(ig_ref, per, None)
-    spread = (lax.broadcasted_iota(jnp.int32, (16, VC), 1) // HEAD_DIM
-              == lax.broadcasted_iota(jnp.int32, (16, VC), 0)).astype(f32)
-
-    def widen(m):
-        return jnp.dot(m, spread, precision=hi, preferred_element_type=f32)
-
-    skip_wide = widen(heads[:, 0:16])[2:3]
+    spread = (lax.broadcasted_iota(jnp.int32, (48, VC), 1) // HEAD_DIM
+              == lax.rem(lax.broadcasted_iota(jnp.int32, (48, VC), 0), 16)).astype(bf16)
+
+    def thirds(m):
+        top = m.astype(bf16).astype(f32)
+        mid = (m - top).astype(bf16).astype(f32)
+        return [top, mid, m - top - mid]
+
+    def widen(parts):
+        return jnp.dot(parts.astype(bf16), spread, preferred_element_type=f32)
+
+    skip_wide = widen(jnp.concatenate(thirds(heads[:, 0:16]), axis=1))[2:3]
     ii = lax.broadcasted_iota(jnp.int32, (BLOCK, BLOCK), 0)
     jj = lax.broadcasted_iota(jnp.int32, (BLOCK, BLOCK), 1)
     causal = ii >= jj
-    triu = (ii <= jj).astype(f32)
+    triu = (ii <= jj).astype(bf16)
     low_lane = lax.broadcasted_iota(jnp.int32, (BLOCK, 128), 1) < HEAD_DIM
     margin = CONV - 1
 
@@ -446,9 +450,10 @@
             hook()
         raw = lax.dot_general(w_steps, nb, (((1,), (1,)), ((), ())), preferred_element_type=f32) + dtb
         dt_t = jnp.maximum(raw, 0.0) + jnp.log1p(jnp.exp(-jnp.abs(raw)))
-        cum_t = jnp.dot(-dt_t * rate, triu, precision=hi, preferred_element_type=f32)
+        sums = jnp.dot(jnp.concatenate(thirds(-dt_t * rate), axis=0).astype(bf16), triu, preferred_element_type=f32)
+        cum_t = sums[0:16] + (sums[16:32] + sums[32:48])
         tail_t = jnp.exp(cum_t[:, BLOCK - 1 : BLOCK] - cum_t) * dt_t
-        cols = jnp.concatenate([cum_t, tail_t, jnp.exp(cum_t), jnp.zeros((80, BLOCK), f32)], axis=0).T
+        cols = jnp.concatenate([cum_t, *thirds(tail_t), *thirds(jnp.exp(cum_t)), jnp.zeros((16, BLOCK), f32)], axis=0).T
         cum = cols[:, 0:16]
         bm = vbuf[:, VC : VC + STATE]
         cm = vbuf[:, VC + STATE : CC]
@@ -457,8 +462,8 @@
         vals = vbuf[:, 0:VC].astype(f32)
         part = skip_wide * vals
         if h > 0:
-            grow = widen(cols[:, 32:48])
-            part = part + grow * jnp.dot(cm.astype(f32), state[k], precision=hi,
+            grow = widen(cols[:, 64:112])
+            part = part + grow * jnp.dot(jnp.concatenate([cm, cm, cm], axis=1), state[k],
                                          preferred_element_type=f32)
         for p in range(VC // 128):
             mix = []
@@ -474,11 +479,14 @@
             ybuf[:, p * 128 : (p + 1) * 128] = got + part[:, p * 128 : (p + 1) * 128]
         y = ybuf[...]
         pbuf[k, h] = jnp.dot((y * gain_out).astype(bf16), wobuf[...], preferred_element_type=f32).astype(bf16)
-        stbuf[k, h] = lax.dot_general(jnp.ones((8, VC), f32), y * y, (((1,), (1,)), ((), ())),
-                                      precision=hi, preferred_element_type=f32)
+        ones = jnp.ones((8, VC), bf16)
+        stat = [lax.dot_general(ones, sq.astype(bf16), (((1,), (1,)), ((), ())), preferred_element_type=f32)
+                for sq in thirds(y * y)]
+        stbuf[k, h] = stat[0] + (stat[1] + stat[2])
         if h == 0:
-            scaled = (vals * widen(cols[:, 16:32])).astype(bf16)
-            state[k] = lax.dot_general(bm, scaled, (((0,), (0,)), ((), ())), preferred_element_type=f32)
+            scaled = (vals * widen(cols[:, 16:64])).astype(bf16)
+            whole = lax.dot_general(bm, scaled, (((0,), (0,)), ((), ())), preferred_element_type=f32)
+            state[k] = jnp.concatenate(thirds(whole), axis=0).astype(bf16)
 
     def place(b, h):
         return {"dp": b, "seq": h}
@@ -522,8 +530,8 @@
             return (big,)
         return (rcopy(jstat.at[h], rstat.at[S], jt_send.at[h], t_recv.at[S], where), big)
 
-    def join_near(h, chunks=range(QP)):
-        @pl.when(joiner)
+    def join_near(h, chunks=range(QP), on=True):
+        @pl.when(jnp.logical_and(joiner, on))
         def _():
             for q in chunks:
                 at = band(q, QP)
@@ -582,6 +590,12 @@
                         cp.wait_recv()
                 for cp in f_copies(d, c):
                     cp.start()
+    with scope("prewait"):
+        send_x(jnp.logical_and(c == 1, inner), False)
+        pass_at(far, 1, summer)
+        pass_at(near, 1, summer)
+        for q in range(QX):
+            own_on(1, q, lambda cp: cp.start())
     with scope("fwait"):
         for cp in forwards():
             cp.wait_recv()
@@ -625,13 +639,6 @@
             obuf[at, :] = (x_ref[at].astype(f32) + total * scale[q * size : (q + 1) * size]).astype(bf16)
             e_copy(q).start()
 
-    with scope('own1'):
-        pass_at(near, 1, summer)
-        for q in range(QX):
-            own_on(1, q, lambda cp: cp.start())
-
-    with scope("passf1h"):
-        pass_at(far, 1, summer)
     with scope("passn0"):
         pass_at(near, 0, outer)
     with scope("unit0"):
@@ -639,7 +646,6 @@
         unit(one, 0, lambda: pass_at(far, 1, joiner, (0,)))
     with scope("passf1i"):
         pass_at(far, 1, joiner, (1,))
-    send_x(jnp.logical_and(c == 1, inner), False)
     with scope("passf0"):
         pass_at(far, 0, outer)
     with scope("unit1"):
@@ -673,10 +679,13 @@
         @pl.when(c == 0)
         def _():
             finish()
-    with scope("join1"):
-        join_near(1)
-    with scope("sumf1"):
-        sum_far(1, on=joiner)
+    for q in range(QP):
+        with scope("join1"):
+            join_near(1, (q,), jnp.logical_not(upper))
+        with scope("sumf1"):
+            sum_far(1, (q,), joiner)
+        with scope("join1u"):
+            join_near(1, (q,), upper)
     with scope("fin1"):
         @pl.when(c == 1)
         def _():
@@ -749,7 +758,7 @@
             V((VC, D), bf16),
             V((S, 2, rows, D), bf16), V((S, 2, rows, D), bf16),
             V((8 + rows, CC), f32), V((S, 8, CC), f32), V((rows, CC), bf16), V((rows, VC), f32),
-            V((S, STATE, VC), f32),
+            V((S, 3 * STATE, VC), bf16),
             V((S, 2, rows, D), bf16), V((S, 2, 8, rows), f32),
             V((2, rows, D), bf16), V((2, 8, rows), f32),
             V((2, rows, D), bf16), V((2, 8, rows), f32),

time: 69 us -> 67.7 us (0.981); the launches traced: 68.1 us -> 67.5 us
  no operation moved by 1% of the time
where the time goes in v4:
time: 67.7 us; the launch traced here: 67.5 us
  Pallas kernels  66.8 us (99%)
  local copies, waits for them, and re-layouts  0.73 us (1%)
    pallas_call x1, Pallas kernels, fused(): pl.pallas_call(functools.partial(section_kernel, Z), out_shape=jax.ShapeD...  66.8 us

profile of v4, /device:TPU:1, one launch (start us, length us, event | category | flops | bytes accessed | tf_op | source)
XLA Modules:
  0.0 67.5 jit_solution(8863558382116443966)
XLA Ops:
  0.0 66.8 %shard_map.109 = bf16[128,1280]{1,0:T(8,128)(2,1)S(1)} custom-call(bf16[128,1280]{1,0:T(8,128)(2,1)} %bitcast.11, f32[1,1280]{1,0:T(1,128)} %ng_hbm.1, bf16[160,2688]{1,0:T(8,128)(2,1)} %bitcast.9, bf16[40,160]{1,0:T(8,128)(2,1)} %bitcast.13, f32[4,2688]{1,0:T(4,128)} %bitcast.12, f32[1,2688]{1,0:T(1,128)} %cb_hbm.1, f32[1,40]{1,0:T(1,128)} %db_hbm.1, ...), custom_call_target="tpu_custom_call" | custom-call | tf_op jit(solution)/shard_map/pallas_call | solution.py:746
  66.8 0.7 %copy.13 = bf16[1,1,128,1280]{3,2,1,0:T(8,128)(2,1)} copy(bf16[1,1,128,1280]{3,2,1,0:T(8,128)(2,1)S(1)} %bitcast.8) | data formatting | bytes 655360

commit v5 on v4

--- a/solution.py
+++ b/solution.py
@@ -16,8 +16,8 @@
 
 
 epsilon = 1e-05
-QX = 4
-QP = 4
+QX = 2
+QP = 8
 
 
 def prefix(x, axis, combine, identity):
@@ -645,16 +645,16 @@
         norm_in(one, 0)
         unit(one, 0, lambda: pass_at(far, 1, joiner, (0,)))
     with scope("passf1i"):
-        pass_at(far, 1, joiner, (1,))
+        None
     with scope("passf0"):
         pass_at(far, 0, outer)
     with scope("unit1"):
         norm_in(two, 0)
-        unit(two, 0, lambda: pass_at(far, 1, joiner, (2,)))
+        unit(two, 0, lambda: pass_at(far, 1, joiner, (1,)))
     send_far(0)
     send_near(0, outer)
     with scope("passf1j"):
-        pass_at(far, 1, joiner, (3,))
+        None
     with scope("sumf0"):
         sum_far(0)
     with scope("passf1"):

time: 67.7 us -> 67.6 us (level)
  no operation moved by 1% of the time
where the time goes in v5:
time: 67.6 us; the launch traced here: 67.5 us
  Pallas kernels  66.7 us (99%)
  local copies, waits for them, and re-layouts  0.73 us (1%)
    pallas_call x1, Pallas kernels, fused(): pl.pallas_call(functools.partial(section_kernel, Z), out_shape=jax.ShapeD...  66.7 us

profile of v5, /device:TPU:1, one launch (start us, length us, event | category | flops | bytes accessed | tf_op | source)
XLA Modules:
  0.0 67.5 jit_solution(4547037351320758593)
XLA Ops:
  0.0 66.7 %shard_map.109 = bf16[128,1280]{1,0:T(8,128)(2,1)S(1)} custom-call(bf16[128,1280]{1,0:T(8,128)(2,1)} %bitcast.11, f32[1,1280]{1,0:T(1,128)} %ng_hbm.1, bf16[160,2688]{1,0:T(8,128)(2,1)} %bitcast.9, bf16[40,160]{1,0:T(8,128)(2,1)} %bitcast.13, f32[4,2688]{1,0:T(4,128)} %bitcast.12, f32[1,2688]{1,0:T(1,128)} %cb_hbm.1, f32[1,40]{1,0:T(1,128)} %db_hbm.1, ...), custom_call_target="tpu_custom_call" | custom-call | tf_op jit(solution)/shard_map/pallas_call | solution.py:746
  66.7 0.7 %copy.13 = bf16[1,1,128,1280]{3,2,1,0:T(8,128)(2,1)} copy(bf16[1,1,128,1280]{3,2,1,0:T(8,128)(2,1)S(1)} %bitcast.8) | data formatting | bytes 655360
